TPU v7x, 128 devices: a whole 4x4x4 slice. The times are simulated.
128 devices in a mesh: data: 1, cp: 64 (over z, y, x), tp: 2 (over core).
Axes of the slice: x: 4, y: 4, z: 4, core: 2. Of those that a mesh axis runs over, the one named last changes fastest.
Arguments:
- x_in: bfloat16 [16384, 2048], P(('data', 'cp', 'tp'))
- w_q: bfloat16 [2048, 32, 128], P(None, 'tp')
- w_k: bfloat16 [2048, 4, 128], P(None, 'tp')
- w_v: bfloat16 [2048, 4, 128], P(None, 'tp')
- w_o: bfloat16 [32, 128, 2048], P('tp')
- expert_idx: int32 [16384, 2], P(('data', 'cp', 'tp'))
- gate_wts: float32 [16384, 2], P(('data', 'cp', 'tp'))
- w_gate: bfloat16 [128, 2048, 768], P(('cp', 'tp'))
- w_up: bfloat16 [128, 2048, 768], P(('cp', 'tp'))
- w_down: bfloat16 [128, 768, 2048], P(('cp', 'tp'))
Outputs:
- output: bfloat16 [16384, 2048], P(('data', 'cp', 'tp'))
All inputs are finite; a program needn't handle non-finite values.
Results may differ from a plain program's by a relative error of at most 0.0101173.
Values are sent between devices in bfloat16 or wider.
A program may use at most 1 GiB of HBM per device.

v0:
```python
import jax
import jax.numpy as jnp
from jax import lax
from jax.sharding import PartitionSpec as P


def row_positions(cp_ranks, cp_size, tp_size, tok_dev):
    half_rows = tok_dev // 2
    local_rows = jnp.arange(tp_size * tok_dev)
    tp_src = local_rows // tok_dev
    within = local_rows % tok_dev
    seg_index = jnp.where((within < half_rows)[None, :], cp_ranks[:, None], 2 * cp_size - 1 - cp_ranks[:, None])
    offset = tp_src * half_rows + within % half_rows
    return (seg_index * (tp_size * half_rows) + offset[None, :]).reshape(-1)


def solution(mesh):
    cp_size = mesh.shape['cp']
    tp_size = mesh.shape['tp']
    num_devs = cp_size * tp_size
    row_spec = P(('data', 'cp', 'tp'), None)
    head_spec = P(None, 'tp', None)
    wo_spec = P('tp', None, None)
    expert_spec = P(('cp', 'tp'), None, None)

    def device_fn(x_blk, w_q, w_k, w_v, w_o, idx_blk, gate_blk, w_gate, w_up, w_down):
        tok_dev = x_blk.shape[0]
        kv_local, head_dim = w_k.shape[1], w_k.shape[2]
        q_per_kv = w_q.shape[1] // kv_local
        exp_local = w_gate.shape[0]
        num_exp = exp_local * num_devs
        capacity = 4 * tok_dev // num_exp
        cp_rank = lax.axis_index('cp')

        x_rows = lax.all_gather(x_blk, 'tp', axis=0, tiled=True)
        queries = jnp.einsum('sm,mnc->snc', x_rows, w_q, preferred_element_type=jnp.float32).astype(jnp.bfloat16)
        keys_loc = jnp.einsum('sm,mnc->snc', x_rows, w_k, preferred_element_type=jnp.float32).astype(jnp.bfloat16)
        vals_loc = jnp.einsum('sm,mnc->snc', x_rows, w_v, preferred_element_type=jnp.float32).astype(jnp.bfloat16)
        keys_all = lax.all_gather(keys_loc, 'cp', axis=0, tiled=True)
        vals_all = lax.all_gather(vals_loc, 'cp', axis=0, tiled=True)
        pos_q = row_positions(cp_rank.reshape(1), cp_size, tp_size, tok_dev)
        pos_k = row_positions(jnp.arange(cp_size), cp_size, tp_size, tok_dev)
        q_grp = queries.reshape(-1, kv_local, q_per_kv, head_dim)
        scores = jnp.einsum('qngc,knc->ngqk', q_grp, keys_all, preferred_element_type=jnp.float32) * (head_dim ** -0.5)
        scores = jnp.where(pos_k[None, None, None, :] <= pos_q[None, None, :, None], scores, -jnp.inf)
        exp_scores = jnp.exp(scores - jnp.max(scores, axis=-1, keepdims=True))
        attn_prob = (exp_scores / jnp.sum(exp_scores, axis=-1, keepdims=True)).astype(jnp.bfloat16)
        head_out = jnp.einsum('ngqk,knc->qngc', attn_prob, vals_all, preferred_element_type=jnp.float32).astype(jnp.bfloat16)
        part_sum = jnp.einsum('qngc,ngcm->qm', head_out, w_o.reshape(kv_local, q_per_kv, head_dim, -1), preferred_element_type=jnp.float32)
        attn_out = lax.psum_scatter(part_sum, 'tp', scatter_dimension=0, tiled=True)
        hidden = (x_blk.astype(jnp.float32) + attn_out).astype(jnp.bfloat16)

        flat_ids = idx_blk.reshape(-1)
        onehot = (flat_ids[:, None] == jnp.arange(num_exp)[None, :]).astype(jnp.int32)
        slot_pos = jnp.sum(jnp.cumsum(onehot, axis=0) * onehot, axis=1) - 1
        slot_ids = (flat_ids * capacity + slot_pos).reshape(tok_dev, 2)
        select = (slot_ids[:, :, None] == jnp.arange(num_exp * capacity)[None, None, :]).astype(jnp.bfloat16)
        send_buf = jnp.einsum('tkn,tm->nm', select, hidden, preferred_element_type=jnp.float32).astype(jnp.bfloat16)
        recv_buf = lax.all_to_all(send_buf, ('cp', 'tp'), 0, 0, tiled=True)
        tok_in = recv_buf.reshape(num_devs, exp_local, capacity, -1)
        gate_pre = jnp.einsum('secm,emf->secf', tok_in, w_gate, preferred_element_type=jnp.float32)
        up_pre = jnp.einsum('secm,emf->secf', tok_in, w_up, preferred_element_type=jnp.float32)
        hid_act = (jax.nn.silu(gate_pre) * up_pre).astype(jnp.bfloat16)
        exp_out = jnp.einsum('secf,efm->secm', hid_act, w_down, preferred_element_type=jnp.float32).astype(jnp.bfloat16)
        back_buf = lax.all_to_all(exp_out.reshape(num_devs * exp_local * capacity, -1), ('cp', 'tp'), 0, 0, tiled=True)
        picked = jnp.einsum('tkn,nm->tkm', select, back_buf, preferred_element_type=jnp.float32)
        moe_out = jnp.sum(gate_blk[:, :, None] * picked, axis=1)
        return (hidden.astype(jnp.float32) + moe_out).astype(jnp.bfloat16)

    return jax.shard_map(device_fn, mesh=mesh, in_specs=(row_spec, head_spec, head_spec, head_spec, wo_spec, row_spec, row_spec, expert_spec, expert_spec, expert_spec), out_specs=row_spec, check_vma=False)
```

profile of v0, /device:TPU:1, one launch (start us, length us, event | category | flops | bytes accessed | tf_op | source)
XLA Modules:
  0.0 615.6 jit_solution(10078530340096804117)
XLA Ops:
  6.5 0.0 copy-start
  6.5 0.7 all-gather.4.cloned.1.call-update
  7.3 0.0 all-gather.8.cloned.1.call-start
  7.3 16.9 %all-gather.4.cloned.1.call-done = bf16[256,2048]{1,0:T(8,128)(2,1)} async-done(((bf16[128,2048]{1,0:T(8,128)(2,1)}), bf16[256,2048]{1,0:T(8,128)(2,1)}) %all-gather.4.cloned.1.call-update) | async-done | bytes 1048592 | tf_op jit(solution)/shard_map/all_gather | solution.py:35
  24.2 2.6 convolution_convert_fusion.1
  26.9 0.0 all-gather.8.cloned.1.call-update
  26.9 0.0 all-gather.6.cloned.1.call-start
  27.0 0.1 add_bitcast_fusion
  27.1 0.0 copy-start.5
  27.1 0.0 copy-start.6
  27.2 8.2 %broadcast_compare_fusion = pred[256,16384]{0,1:T(8,128)(4,1)} fusion(s32[256]{0:T(256)S(1)} %multiply_add_fusion.1, s32[16384]{0:T(1024)S(1)} %bitcast.125), kind=kLoop, calls=%fused_computation.14 | loop fusion | flops 4194304 | bytes 4260864 | tf_op jit(solution)/shard_map/le | solution.py:45
  35.4 0.4 convolution_convert_fusion.2
  35.8 0.8 copy.44
  36.6 0.0 all-gather.6.cloned.1.call-update
  36.6 0.0 reduce-scatter.2.cloned.1.call-start
  36.7 7.1 %fusion.34 = bf16[256,16,128]{2,0,1:T(8,128)(2,1)} fusion(bf16[2048,16,128]{2,1,0:T(8,128)(2,1)} %param.11, bf16[256,2048]{1,0:T(8,128)(2,1)} %all-gather.4.cloned.1.call-done), kind=kOutput, calls=%fused_computation.35 | convolution fusion | flops 2148007936 | bytes 10485760 | tf_op jit(solution)/shard_map/sm,mnc->snc/dot_general | solution.py:36
  43.7 62.8 %all-gather.8.cloned.1.call-done = bf16[16384,2,128]{2,0,1:T(8,128)(2,1)} async-done(((bf16[256,2,128]{2,0,1:T(8,128)(2,1)}), bf16[16384,2,128]{2,0,1:T(8,128)(2,1)}) %all-gather.8.cloned.1.call-update) | async-done | bytes 8388624 | tf_op jit(solution)/shard_map/all_gather | solution.py:39
  106.5 90.6 %fusion.1 = (f32[2,8,256]{2,1,0:T(8,128)S(1)}, f32[2,16384,256,8]{2,1,3,0:T(8,128)}) fusion(pred[256,16384]{0,1:T(8,128)(4,1)} %broadcast_compare_fusion, bf16[256,2,8,128]{3,0,2,1:T(8,128)(2,1)} %bitcast.128, bf16[16384,2,128]{2,0,1:T(8,128)(2,1)} %all-gather.8.cloned.1.call-done), kind=kOutput, calls=%fused_computation.4 | convolution fusion | flops 17381191680 | bytes 282083328 | tf_op jit(solution)/shard_map/qngc,knc->ngqk/dot_general | solution.py:44
  197.2 81.9 %fusion = f32[2,8,256]{2,1,0:T(8,128)S(1)} fusion(f32[2,16384,256,8]{2,1,3,0:T(8,128)} %get-tuple-element.6, f32[2,8,256]{2,1,0:T(8,128)S(1)} %get-tuple-element.5, pred[256,16384]{0,1:T(8,128)(4,1)} %broadcast_compare_fusion), kind=kLoop, calls=%fused_computation.3 | loop fusion | flops 268431360 | bytes 272662528 | tf_op jit(solution)/shard_map/reduce_sum | solution.py:47
  279.1 129.2 %divide_convert_fusion = bf16[2,8,256,16384]{2,3,1,0:T(8,128)(2,1)} fusion(f32[2,16384,256,8]{2,1,3,0:T(8,128)} %get-tuple-element.6, f32[2,8,256]{2,1,0:T(8,128)S(1)} %fusion, f32[2,8,256]{2,1,0:T(8,128)S(1)} %get-tuple-element.5, pred[256,16384]{0,1:T(8,128)(4,1)} %broadcast_compare_fusion), kind=kLoop, calls=%fused_computation.1 | loop fusion | flops 335544320 | bytes 406880256 | tf_op jit(solution)/shard_map/convert_element_type | solution.py:47
  408.3 0.0 all-gather.6.cloned.1.call-done
  408.3 21.2 %copy.47 = bf16[16384,2,128]{0,2,1:T(8,128)(2,1)} copy(bf16[16384,2,128]{2,1,0:T(2,128)(2,1)} %all-gather.6.cloned.1.call-done) | data formatting | bytes 16777216 | tf_op jit(solution)/shard_map/all_gather | solution.py:40
  429.5 45.7 %fusion.42.clone.4 = bf16[256,2,8,128]{0,3,1,2:T(8,128)(2,1)} fusion(bf16[2,8,256,16384]{2,3,1,0:T(8,128)(2,1)} %divide_convert_fusion, bf16[16384,2,128]{0,2,1:T(8,128)(2,1)} %copy.47), kind=kOutput, calls=%fused_computation.37.clone.clone.clone.1 | convolution fusion | flops 17180393472 | bytes 143654912 | tf_op jit(solution)/shard_map/ngqk,knc->qngc/dot_general | solution.py:48
  475.2 7.4 %fusion.20 = f32[256,2048]{1,0:T(8,128)} fusion(bf16[2,8,128,2048]{3,2,1,0:T(8,128)(2,1)} %bitcast.127, bf16[256,2,8,128]{0,3,1,2:T(8,128)(2,1)} %fusion.42.clone.4), kind=kOutput, calls=%fused_computation.23 | convolution fusion | flops 2147483648 | bytes 11534336 | tf_op jit(solution)/shard_map/qngc,ngcm->qm/dot_general | solution.py:49
  482.7 0.0 reduce-scatter.2.cloned.1.call-update
  482.7 0.1 copy.51
  482.8 0.1 eq.47
  482.9 0.1 eq.43
  483.1 0.1 copy.53
  483.2 0.2 fusion.68
  483.5 0.2 fusion.69
  483.7 0.1 sub.46
  483.8 0.1 copy.55
  483.9 0.1 convert_reduce_fusion
  484.1 11.1 %reduce-scatter.2.cloned.1.call-done = f32[128,2048]{1,0:T(8,128)} async-done(((f32[256,2048]{1,0:T(8,128)}), f32[128,2048]{1,0:T(8,128)}) %reduce-scatter.2.cloned.1.call-update) | async-done | bytes 1048592 | tf_op jit(solution)/shard_map/reduce_scatter | solution.py:50
  495.1 3.4 convolution_convert_fusion
  498.6 4.1 all_to_all.12
  502.7 43.4 %all_to_all.18 = bf16[128,4,2048]{2,1,0:T(4,128)(2,1)S(1)} all-to-all(bf16[128,4,2048]{2,1,0:T(4,128)(2,1)} %all_to_all.12), channel_id=1, replica_groups=mesh['data'=1,'cp'=64,'tp'=2] {'cp','tp'}, dimensions={0} | all-to-all | bytes 4194304 | tf_op jit(solution)/shard_map/all_to_all | solution.py:59
  546.1 1.3 copy-done.2
  547.4 4.8 fusion.15
  552.2 9.8 %fusion.17 = bf16[128,4,2048]{2,0,1:T(8,128)(2,1)} fusion(bf16[1,768,2048]{2,1,0:T(8,128)(2,1)S(1)} %copy-done, bf16[1,2048,768]{2,1,0:T(8,128)(2,1)} %param.18, bf16[128,4,2048]{2,1,0:T(4,128)(2,1)} %copy-done.2, f32[128,4,768]{2,0,1:T(8,128)} %fusion.15), kind=kOutput, calls=%fused_computation.22 | convolution fusion | flops 3224633344 | bytes 12058624 | tf_op jit(solution)/shard_map/secf,efm->secm/dot_general | solution.py:64
  562.0 3.2 copy.58
  565.2 0.0 copy-start.7
  565.2 35.2 %all_to_all.19 = bf16[128,4,2048]{2,1,0:T(4,128)(2,1)} all-to-all(bf16[128,4,2048]{2,1,0:T(4,128)(2,1)S(1)} %copy.58), channel_id=1, replica_groups=mesh['data'=1,'cp'=64,'tp'=2] {'cp','tp'}, dimensions={0} | all-to-all | bytes 4194304 | tf_op jit(solution)/shard_map/all_to_all | solution.py:65
  600.5 4.0 reshape.232
  604.4 0.0 copy-done.7
  604.4 2.6 fusion.29
  607.0 2.0 add_convert_fusion
  (24 shorter events, 0.2 us)
Async XLA Ops:
  6.5 545.7 %copy-start = (bf16[1,768,2048]{2,1,0:T(8,128)(2,1)S(1)}, bf16[1,768,2048]{2,1,0:T(8,128)(2,1)}, u32[]{:S(2)}) copy-start(bf16[1,768,2048]{2,1,0:T(8,128)(2,1)} %param.19) | copy-start | bytes 9437188
  6.5 17.7 %all-gather.4.cloned.1.call-start = ((), (), s32[]{:S(2)}) async-start(), calls=%async_computation.3 | async-start | bytes 1572864 | tf_op jit(solution)/shard_map/all_gather | solution.py:35
  7.3 99.3 %all-gather.8.cloned.1.call-start = ((), (), s32[]{:S(2)}) async-start(), calls=%async_computation.5 | async-start | bytes 8519680 | tf_op jit(solution)/shard_map/all_gather | solution.py:39
  26.9 381.4 %all-gather.6.cloned.1.call-start = ((), (), s32[]{:S(2)}) async-start(), calls=%async_computation.4 | async-start | bytes 8519680 | tf_op jit(solution)/shard_map/all_gather | solution.py:40
  27.1 8.2 %copy-start.5 = (bf16[2048,2,128]{2,1,0:T(2,128)(2,1)S(1)}, bf16[2048,2,128]{2,1,0:T(2,128)(2,1)}, u32[]{:S(2)}) copy-start(bf16[2048,2,128]{2,1,0:T(2,128)(2,1)} %param.13) | copy-start | bytes 3145732
  27.1 8.2 %copy-start.6 = (bf16[256,2048]{1,0:T(8,128)(2,1)S(1)}, bf16[256,2048]{1,0:T(8,128)(2,1)}, u32[]{:S(2)}) copy-start(bf16[256,2048]{1,0:T(8,128)(2,1)} %all-gather.4.cloned.1.call-done) | copy-start | bytes 3145732
  36.6 458.5 %reduce-scatter.2.cloned.1.call-start = ((), (), s32[]{:S(2)}) async-start(), calls=%async_computation.6 | async-start | bytes 3145728 | tf_op jit(solution)/shard_map/reduce_scatter | solution.py:50
  475.2 7.5 %copy-start.3 = (s32[128,2]{0,1:T(2,128)S(1)}, s32[128,2]{0,1:T(2,128)}, u32[]{:S(2)}) copy-start(s32[128,2]{0,1:T(2,128)} %param.15) | copy-start | bytes 3076
  502.7 44.8 %copy-start.4 = (bf16[1,2048,768]{2,1,0:T(8,128)(2,1)S(1)}, bf16[1,2048,768]{2,1,0:T(8,128)(2,1)}, u32[]{:S(2)}) copy-start(bf16[1,2048,768]{2,1,0:T(8,128)(2,1)} %param.17) | copy-start | bytes 9437188
  546.1 1.4 copy-start.2
  565.2 39.2 %copy-start.7 = (f32[128,2]{0,1:T(2,128)S(1)}, f32[128,2]{0,1:T(2,128)}, u32[]{:S(2)}) copy-start(f32[128,2]{0,1:T(2,128)} %param.16) | copy-start | bytes 3076
  604.4 2.6 copy-start.1
Sparse Core Ops, SparseCore 0:
  9.0 15.2 all-gather.3
  27.1 79.3 all-gather.7
  109.4 77.6 all-gather.5
  482.8 12.2 reduce-scatter.1
where the time goes:
time: 617 us; the launch traced here: 616 us
  other arithmetic  222 us (36%)
  matrix products  175 us (28%)
  waiting for transfers between devices  91.5 us (15%)
  blocking collectives  78.6 us (13%)
  local copies, waits for them, and re-layouts  35.5 us (6%)
  between operations  13.3 us (2%)
    convert_element_type x1, other arithmetic, device_fn(): (exp_scores / jnp.sum(exp_scores, axis=-1, keepdims=True)).astype(jnp.bfl...  129 us
    dot_general x1, matrix products, device_fn(): jnp.einsum('qngc,knc->ngqk', q_grp, keys_all, preferred_element_type=jnp....  90.6 us
    reduce_sum x1, other arithmetic, device_fn(): jnp.sum(exp_scores, axis=-1, keepdims=True)  81.9 us
    all_gather x1, waiting for transfers between devices, device_fn(): keys_all = lax.all_gather(keys_loc, 'cp', axis=0, tiled=True)  62.8 us
    dot_general x1, matrix products, device_fn(): jnp.einsum('ngqk,knc->qngc', attn_prob, vals_all, preferred_element_type=...  45.7 us
    all_to_all x1, blocking collectives, device_fn(): recv_buf = lax.all_to_all(send_buf, ('cp', 'tp'), 0, 0, tiled=True)  43.4 us
    all_to_all x1, blocking collectives, device_fn(): lax.all_to_all(exp_out.reshape(num_devs * exp_local * capacity, -1), ('cp...  35.2 us
    all_gather x1, local copies, waits for them, and re-layouts, device_fn(): vals_all = lax.all_gather(vals_loc, 'cp', axis=0, tiled=True)  21.2 us
  transfers between devices with their start and end apart: 4, of which 3 were waited for; matrix products, arithmetic and copies ran while one was open for 52% of the time, Pallas kernels for 0%

commit v1 on v0

v1 whole, which is shorter than its diff:
```python
import functools
import math

import jax
import jax.numpy as jnp
from jax import lax
from jax.experimental import pallas as pl
from jax.experimental.pallas import tpu as pltpu
from jax.sharding import PartitionSpec as P

NEG = -1e30
MESH = pl.DeviceIdType.MESH
STEPS = (1, 3, 2)


def swap_kernel(x_ref, o_ref, buf, ssem, rsem):
    cp, tp = lax.axis_index('cp'), lax.axis_index('tp')
    peer = (0, cp, 1 - tp)
    rows = x_ref.shape[0]
    barrier = pltpu.get_barrier_semaphore()
    pl.semaphore_signal(barrier, inc=1, device_id=peer, device_id_type=MESH)
    pl.semaphore_wait(barrier, 1)
    copy = pltpu.make_async_remote_copy(src_ref=x_ref, dst_ref=buf, send_sem=ssem, recv_sem=rsem, device_id=peer, device_id_type=MESH)
    copy.start()
    o_ref[pl.ds(pl.multiple_of(tp * rows, rows), rows), :] = x_ref[...]
    copy.wait()
    o_ref[pl.ds(pl.multiple_of((1 - tp) * rows, rows), rows), :] = buf[...]


def swap_rows(x):
    rows, cols = x.shape
    return pl.pallas_call(
        swap_kernel,
        out_shape=jax.ShapeDtypeStruct((2 * rows, cols), x.dtype),
        in_specs=[pl.BlockSpec(memory_space=pltpu.VMEM)],
        out_specs=pl.BlockSpec(memory_space=pltpu.VMEM),
        scratch_shapes=[pltpu.VMEM((rows, cols), x.dtype), pltpu.SemaphoreType.DMA, pltpu.SemaphoreType.DMA],
        compiler_params=pltpu.CompilerParams(collective_id=1, has_side_effects=True),
        name='swap_rows',
    )(x)


def join_kernel(p_ref, x_ref, o_ref, buf, ssem, rsem):
    cp, tp = lax.axis_index('cp'), lax.axis_index('tp')
    peer = (0, cp, 1 - tp)
    rows = x_ref.shape[0]
    barrier = pltpu.get_barrier_semaphore()
    pl.semaphore_signal(barrier, inc=1, device_id=peer, device_id_type=MESH)
    pl.semaphore_wait(barrier, 1)
    away = p_ref.at[pl.ds(pl.multiple_of((1 - tp) * rows, rows), rows)]
    copy = pltpu.make_async_remote_copy(src_ref=away, dst_ref=buf, send_sem=ssem, recv_sem=rsem, device_id=peer, device_id_type=MESH)
    copy.start()
    copy.wait()
    mine = p_ref[pl.ds(pl.multiple_of(tp * rows, rows), rows), :]
    o_ref[...] = (x_ref[...].astype(jnp.float32) + (mine + buf[...])).astype(o_ref.dtype)


def join_parts(part, x):
    return pl.pallas_call(
        join_kernel,
        out_shape=jax.ShapeDtypeStruct(x.shape, x.dtype),
        in_specs=[pl.BlockSpec(memory_space=pltpu.VMEM)] * 2,
        out_specs=pl.BlockSpec(memory_space=pltpu.VMEM),
        scratch_shapes=[pltpu.VMEM(x.shape, jnp.float32), pltpu.SemaphoreType.DMA, pltpu.SemaphoreType.DMA],
        compiler_params=pltpu.CompilerParams(collective_id=2, has_side_effects=True),
        name='join_parts',
    )(part, x)


def ring_step(i):
    return 1 + 2 * i - 3 * (i // 2)


def attn_kernel(scale2, q_ref, kt_ref, v_ref, o_ref, qb, kb, vb, so, ob, acc_s, m_s, l_s,
                q_ss, k_ss, v_ss, o_ss, q_rs, kx_rs, vx_rs, o_rs, k_rs, v_rs, kp_rs, vp_rs, kd_ss, vd_ss, kf_ss, vf_ss, kp_ss, vp_ss):
    cp, c = lax.axis_index('cp'), lax.axis_index('tp')
    x, y, z = cp % 4, (cp // 4) % 4, cp // 16
    g = z * 4 + y
    seg = kt_ref.shape[-1]
    half = seg // 2
    wide = so.shape[-1]
    heads = wide // 128

    def dev(xx, yy, zz, t):
        return (0, (zz % 4) * 16 + (yy % 4) * 4 + xx % 4, t)

    barrier = pltpu.get_barrier_semaphore()
    for d in STEPS:
        for t in range(2):
            pl.semaphore_signal(barrier, inc=1, device_id=dev(x + d, y, z, t), device_id_type=MESH)
        pl.semaphore_signal(barrier, inc=1, device_id=dev(x, y + d, z, c), device_id_type=MESH)
        pl.semaphore_signal(barrier, inc=1, device_id=dev(x, y, z + d, c), device_id_type=MESH)
    pl.semaphore_signal(barrier, inc=1, device_id=dev(x, y, z, 1 - c), device_id_type=MESH)
    pl.semaphore_wait(barrier, 13)

    def move(src, dst, ssem, rsem, xx, t, start):
        here = (xx == x) & (t == c)
        far = pltpu.make_async_remote_copy(src_ref=src, dst_ref=dst, send_sem=ssem, recv_sem=rsem, device_id=dev(xx, y, z, t), device_id_type=MESH)

        @pl.when(jnp.logical_not(here))
        def _():
            if start:
                far.start()
            else:
                far.wait_send()

        if start:
            @pl.when(here)
            def _():
                pltpu.make_async_copy(src, dst, rsem).start()

    def exchange(start):
        for j in range(2):
            for t in range(2):
                i = j * 2 + t
                move(kt_ref.at[j, t], kb.at[t, g, x], k_ss.at[i], kx_rs, 2 * c + j, t, start)
                move(v_ref.at[j, t], vb.at[t, g, x], v_ss.at[i], vx_rs, 2 * c + j, t, start)
        for j in range(2):
            for t in range(2):
                i = j * 2 + t
                move(q_ref.at[:, pl.ds(i * wide, wide)], qb.at[x], q_ss.at[i], q_rs, 2 * c + j, t, start)

    def arrived(ref, sem):
        pltpu.make_async_copy(ref, ref, sem).wait()

    def push(buf, gg, yy, zz, t, ssem, rsem):
        pltpu.make_async_remote_copy(src_ref=buf.at[c, gg], dst_ref=buf.at[c, gg], send_sem=ssem, recv_sem=rsem.at[gg], device_id=dev(x, yy, zz, t), device_id_type=MESH).start()

    def to_partner(gg):
        push(kb, gg, y, z, 1 - c, kp_ss, kp_rs)
        push(vb, gg, y, z, 1 - c, vp_ss, vp_rs)

    exchange(True)
    arrived(kb.at[c, g], kx_rs)
    arrived(vb.at[c, g], vx_rs)
    for d in STEPS:
        push(kb, g, y + d, z, c, kd_ss, k_rs)
        push(vb, g, y + d, z, c, vd_ss, v_rs)
        push(kb, g, y, z + d, c, kd_ss, k_rs)
        push(vb, g, y, z + d, c, vd_ss, v_rs)
        if d == 1:
            to_partner(g)
    arrived(qb, q_rs)

    units = [(hh, xp) for hh in range(heads) for xp in range(2)]
    keys = 4 * seg
    rows = 2 * seg

    def q_unit(qs, hh, xp):
        parts = [qb[xx, pl.ds(pl.multiple_of(t * seg + qs * half, half), half), hh * 128:(hh + 1) * 128] for xx in (2 * xp, 2 * xp + 1) for t in range(2)]
        return jnp.concatenate(parts, axis=0)

    def tiles(gg, work):
        todo = []
        for qs, h, masked, first in work:
            kt = jnp.concatenate([kb[h, gg, i] for i in range(4)], axis=1)
            todo += [(qs, h, masked, first, kt, hh, xp) for hh, xp in units]

        def score(item):
            qs, h, masked, first, kt, hh, xp = item
            return jnp.dot(q_unit(qs, hh, xp), kt, preferred_element_type=jnp.float32)

        s_next = score(todo[0])
        for n, (qs, h, masked, first, kt, hh, xp) in enumerate(todo):
            s = s_next
            if n + 1 < len(todo):
                s_next = score(todo[n + 1])
            if masked:
                col = lax.broadcasted_iota(jnp.int32, (rows, keys), 1)
                row = lax.broadcasted_iota(jnp.int32, (rows, keys), 0) + xp * rows
                ck, cq = col // seg, row // seg
                before = (ck < cq) if h == 0 else (ck > cq)
                s = jnp.where(before | ((ck == cq) & (col % seg <= row % seg)), s, NEG)
            at = pl.ds(xp * rows, rows)
            m_new = jnp.broadcast_to(jnp.max(s, axis=1, keepdims=True) * scale2, (rows, 128))
            if not first:
                m_prev = m_s[qs, hh, at]
                m_new = jnp.maximum(m_prev, m_new)
                alpha = jnp.exp2(m_prev - m_new)
            m_s[qs, hh, at] = m_new
            ps = [jnp.exp2(s[:, i * 128:(i + 1) * 128] * scale2 - m_new) for i in range(4)]
            lp = (ps[0] + ps[1]) + (ps[2] + ps[3])
            p = jnp.concatenate([v.astype(jnp.bfloat16) for v in ps], axis=1)
            val = vb[h, gg].reshape(keys, 128)
            pv = jnp.dot(p, val, preferred_element_type=jnp.float32)
            if first:
                l_s[qs, hh, at] = lp
                acc_s[qs, hh, at] = pv
            else:
                l_s[qs, hh, at] = l_s[qs, hh, at] * alpha + lp
                acc_s[qs, hh, at] = acc_s[qs, hh, at] * alpha + pv

    def ready(gg):
        arrived(kb.at[1 - c, gg], kp_rs.at[gg])
        arrived(vb.at[1 - c, gg], vp_rs.at[gg])

    def later(gg):
        ready(gg)
        h = (gg > g).astype(jnp.int32)
        tiles(gg, [(1, 0, False, False), (h, h, False, False)])

    ready(g)
    tiles(g, [(1, 0, False, True), (0, 0, True, True), (1, 1, True, False)])

    def group(dy, dz):
        return ((z + 4 - dz) % 4) * 4 + (y + 4 - dy) % 4

    def pass_direct(i):
        d = ring_step(i)
        gy, gz = group(d, 0), group(0, d)
        for gg in (gy, gz):
            arrived(kb.at[c, gg], k_rs.at[gg])
            arrived(vb.at[c, gg], v_rs.at[gg])
            to_partner(gg)
        for e in STEPS:
            push(kb, gy, y, z + e, c, kf_ss, k_rs)
            push(vb, gz, y + e, z, c, vf_ss, v_rs)

    def direct(i, _):
        @pl.when(i < 2)
        def _():
            pass_direct(i + 1)
        d = ring_step(i)
        later(group(d, 0))
        later(group(0, d))
        return 0

    pass_direct(0)
    lax.fori_loop(0, 3, direct, 0)

    def corner(i):
        return group(ring_step(i // 3), ring_step(i % 3))

    def pass_corner(i):
        gg = corner(i)
        arrived(kb.at[c, gg], k_rs.at[gg])
        arrived(vb.at[c, gg], v_rs.at[gg])
        to_partner(gg)

    def corners(i, _):
        @pl.when(i < 8)
        def _():
            pass_corner(i + 1)
        later(corner(i))
        return 0

    pass_corner(0)
    lax.fori_loop(0, 9, corners, 0)

    for qs in range(2):
        for hh, xp in units:
            at = pl.ds(xp * rows, rows)
            out = (acc_s[qs, hh, at] / jnp.sum(l_s[qs, hh, at], axis=1, keepdims=True)).astype(so.dtype)
            for n, (xx, t) in enumerate([(xx, t) for xx in (2 * xp, 2 * xp + 1) for t in range(2)]):
                so[xx, t * seg + qs * half:t * seg + (qs + 1) * half, hh * 128:(hh + 1) * 128] = out[n * half:(n + 1) * half]

    def give_back(start):
        for i in range(4):
            cols = pl.ds(pl.multiple_of(((x % 2) * 2 + c) * wide, wide), wide)
            move(so.at[i], ob.at[:, cols], o_ss.at[i], o_rs, i, x // 2, start)

    give_back(True)
    arrived(ob, o_rs)
    o_ref[...] = ob[...]
    give_back(False)
    exchange(False)
    arrived(kb.at[0, pl.ds(0, 6)], kd_ss)
    arrived(vb.at[0, pl.ds(0, 6)], vd_ss)
    arrived(kb.at[0, pl.ds(0, 9)], kf_ss)
    arrived(vb.at[0, pl.ds(0, 9)], vf_ss)
    arrived(kb.at[0], kp_ss)
    arrived(vb.at[0], vp_ss)


def attention(q, kt, val):
    rows, cols = q.shape
    seg = kt.shape[-1]
    wide = cols // 4
    dma = pltpu.SemaphoreType.DMA
    bf, f32 = jnp.bfloat16, jnp.float32
    return pl.pallas_call(
        functools.partial(attn_kernel, (128 ** -0.5) * math.log2(math.e)),
        out_shape=jax.ShapeDtypeStruct((rows, cols), bf),
        in_specs=[pl.BlockSpec(memory_space=pltpu.VMEM)] * 3,
        out_specs=pl.BlockSpec(memory_space=pltpu.VMEM),
        scratch_shapes=[
            pltpu.VMEM((4, rows, wide), bf),
            pltpu.VMEM((2, 16, 4, seg, 128), bf),
            pltpu.VMEM((2, 16, 4, seg, 128), bf),
            pltpu.VMEM((4, rows, wide), bf),
            pltpu.VMEM((rows, cols), bf),
            pltpu.VMEM((2, wide // 128, 4 * seg, 128), f32),
            pltpu.VMEM((2, wide // 128, 4 * seg, 128), f32),
            pltpu.VMEM((2, wide // 128, 4 * seg, 128), f32),
            dma((4,)), dma((4,)), dma((4,)), dma((4,)),
            dma, dma, dma, dma,
            dma((16,)), dma((16,)), dma((16,)), dma((16,)),
            dma, dma, dma, dma, dma, dma,
        ],
        compiler_params=pltpu.CompilerParams(collective_id=3, has_side_effects=True, vmem_limit_bytes=48 * 1024 * 1024),
        name='ring_attention',
    )(q, kt, val)


def solution(mesh):
    cp_size = mesh.shape['cp']
    tp_size = mesh.shape['tp']
    num_devs = cp_size * tp_size
    row_spec = P(('data', 'cp', 'tp'), None)
    head_spec = P(None, 'tp', None)
    wo_spec = P('tp', None, None)
    expert_spec = P(('cp', 'tp'), None, None)

    def device_fn(x_blk, w_q, w_k, w_v, w_o, idx_blk, gate_blk, w_gate, w_up, w_down):
        tok_dev, d_model = x_blk.shape
        half = tok_dev // 2
        exp_local = w_gate.shape[0]
        num_exp = exp_local * num_devs
        capacity = 4 * tok_dev // num_exp

        x_rows = swap_rows(x_blk)
        x_seg = x_rows.reshape(2, 2, half, d_model).swapaxes(0, 1).reshape(2, tok_dev, d_model)
        key_t = jnp.einsum('mnc,hsm->nhcs', w_k, x_seg, preferred_element_type=jnp.float32).astype(jnp.bfloat16)
        val = jnp.einsum('hsm,mnc->nhsc', x_seg, w_v, preferred_element_type=jnp.float32).astype(jnp.bfloat16)
        queries = jnp.dot(x_rows, w_q.reshape(d_model, -1), preferred_element_type=jnp.float32).astype(jnp.bfloat16)
        head_out = attention(queries, key_t, val)
        part_sum = jnp.dot(head_out, w_o.reshape(-1, d_model), preferred_element_type=jnp.float32)
        hidden = join_parts(part_sum, x_blk)

        flat_ids = idx_blk.reshape(-1)
        onehot = (flat_ids[:, None] == jnp.arange(num_exp)[None, :]).astype(jnp.int32)
        slot_pos = jnp.sum(jnp.cumsum(onehot, axis=0) * onehot, axis=1) - 1
        slot_ids = (flat_ids * capacity + slot_pos).reshape(tok_dev, 2)
        select = (slot_ids[:, :, None] == jnp.arange(num_exp * capacity)[None, None, :]).astype(jnp.bfloat16)
        send_buf = jnp.einsum('tkn,tm->nm', select, hidden, preferred_element_type=jnp.float32).astype(jnp.bfloat16)
        recv_buf = lax.all_to_all(send_buf, ('cp', 'tp'), 0, 0, tiled=True)
        tok_in = recv_buf.reshape(num_devs, exp_local, capacity, -1)
        gate_pre = jnp.einsum('secm,emf->secf', tok_in, w_gate, preferred_element_type=jnp.float32)
        up_pre = jnp.einsum('secm,emf->secf', tok_in, w_up, preferred_element_type=jnp.float32)
        hid_act = (jax.nn.silu(gate_pre) * up_pre).astype(jnp.bfloat16)
        exp_out = jnp.einsum('secf,efm->secm', hid_act, w_down, preferred_element_type=jnp.float32).astype(jnp.bfloat16)
        back_buf = lax.all_to_all(exp_out.reshape(num_devs * exp_local * capacity, -1), ('cp', 'tp'), 0, 0, tiled=True)
        picked = jnp.einsum('tkn,nm->tkm', select, back_buf, preferred_element_type=jnp.float32)
        moe_out = jnp.sum(gate_blk[:, :, None] * picked, axis=1)
        return (hidden.astype(jnp.float32) + moe_out).astype(jnp.bfloat16)

    return jax.shard_map(device_fn, mesh=mesh, in_specs=(row_spec, head_spec, head_spec, head_spec, wo_spec, row_spec, row_spec, expert_spec, expert_spec, expert_spec), out_specs=row_spec, check_vma=False)
```

time: 617 us -> 227 us (0.37)
  other arithmetic: 222 us -> 2.18 us
  matrix products: 175 us -> 31.1 us
  Pallas kernels: 0 us -> 100 us
  waiting for transfers between devices: 91.5 us -> 0 us
  local copies, waits for them, and re-layouts: 35.5 us -> 16 us
  between operations: 13.3 us -> 0.19 us
    dot_general x6 -> x4, matrix products: 154 us -> 10.8 us  [the longest x1 6.14 us: device_fn(): jnp.dot(x_rows, w_q.reshape(d_model, -1), preferred_element_type=jnp.floa...]
    convert_element_type x1 -> x0, other arithmetic: 129 us -> none  [device_fn(): (exp_scores / jnp.sum(exp_scores, axis=-1, keepdims=True)).astype(jnp.bfl...]
    pallas_call x0 -> x3, Pallas kernels: none -> 100 us  [the longest x1 89.9 us: attention(): pl.pallas_call(functools.partial(attn_kernel, 128 ** (-0.5) * math.log2(m...]
    reduce_sum x1 -> x0, other arithmetic: 81.9 us -> none  [device_fn(): jnp.sum(exp_scores, axis=-1, keepdims=True)]
    all_gather x3 -> x0, waiting for transfers between devices: 79.7 us -> none  [the longest x1 62.8 us: device_fn(): keys_all = lax.all_gather(keys_loc, 'cp', axis=0, tiled=True)]
    all_gather x1 -> x0, local copies, waits for them, and re-layouts: 21.2 us -> none  [device_fn(): vals_all = lax.all_gather(vals_loc, 'cp', axis=0, tiled=True)]
    reduce_scatter x1 -> x0, waiting for transfers between devices: 11.1 us -> none  [device_fn(): attn_out = lax.psum_scatter(part_sum, 'tp', scatter_dimension=0, tiled=True)]
    le x1 -> x0, other arithmetic: 8.2 us -> none  [device_fn(): pos_k[None, None, None, :] <= pos_q[None, None, :, None]]
  transfers between devices with their start and end apart: 4 -> 0, of which waited for: 3 -> 0; matrix products, arithmetic and copies ran while one was open for 52% -> 0% of each run, Pallas kernels for 0% -> 0%
where the time goes in v1:
time: 227 us; the launch traced here: 226 us
  Pallas kernels  100 us (44%)
  blocking collectives  76.7 us (34%)
  matrix products  31.1 us (14%)
  local copies, waits for them, and re-layouts  16 us (7%)
    pallas_call x1, Pallas kernels, attention(): pl.pallas_call(functools.partial(attn_kernel, 128 ** (-0.5) * math.log2(m...  89.9 us
    all_to_all x1, blocking collectives, device_fn(): recv_buf = lax.all_to_all(send_buf, ('cp', 'tp'), 0, 0, tiled=True)  39.7 us
    all_to_all x1, blocking collectives, device_fn(): lax.all_to_all(exp_out.reshape(num_devs * exp_local * capacity, -1), ('cp...  37 us
    dot_general x1, matrix products, device_fn(): jnp.einsum('secf,efm->secm', hid_act, w_down, preferred_element_type=jnp....  9.8 us
    dot_general x1, matrix products, device_fn(): jnp.dot(x_rows, w_q.reshape(d_model, -1), preferred_element_type=jnp.floa...  6.14 us
    pallas_call x1, Pallas kernels, join_parts(): pl.pallas_call(join_kernel, out_shape=jax.ShapeDtypeStruct(x.shape, x.dty...  5.28 us
    pallas_call x1, Pallas kernels, swap_rows(): pl.pallas_call(swap_kernel, out_shape=jax.ShapeDtypeStruct((2 * rows, col...  4.98 us
    dot_general x1, matrix products, device_fn(): jnp.einsum('secm,emf->secf', tok_in, w_gate, preferred_element_type=jnp.f...  4.77 us

profile of v1, /device:TPU:1, one launch (start us, length us, event | category | flops | bytes accessed | tf_op | source)
XLA Modules:
  0.0 226.3 jit_solution(8602816244953889018)
XLA Ops:
  0.0 0.0 copy-start
  0.0 0.9 copy.42
  0.9 0.1 eq.42
  1.1 0.1 eq.38
  1.2 0.1 copy.44
  1.3 0.2 fusion.42
  1.6 0.2 fusion.43
  1.8 0.1 sub.7
  2.0 0.1 copy.46
  2.0 0.7 multiply_add_fusion
  2.7 0.1 convert_reduce_fusion
  2.9 5.0 %swap_rows.1 = bf16[256,2048]{1,0:T(8,128)(2,1)} custom-call(bf16[128,2048]{1,0:T(8,128)(2,1)} %x_ref.3), custom_call_target="tpu_custom_call" | custom-call | tf_op jit(solution)/shard_map/swap_rows/pallas_call | solution.py:32
  7.9 0.0 copy-start.5
  7.9 0.0 copy-start.6
  7.9 1.5 copy.37
  9.4 0.0 copy-done.5
  9.4 0.0 copy-start.2
  9.4 0.4 fusion.32.v_ref
  9.9 0.0 copy-done.6
  9.9 0.0 slice-start
  9.9 0.6 fusion.31.kt_ref
  10.4 0.3 copy-done.2
  10.7 0.0 slice-start.1
  10.7 6.1 %fusion.12.q_ref = bf16[256,2048]{1,0:T(8,128)(2,1)S(1)} fusion(bf16[256,2048]{1,0:T(8,128)(2,1)S(1)} %copy-done.2, bf16[256,8,16,128]{3,2,1,0:T(8,128)(2,1)} %bitcast.101), kind=kOutput, calls=%fused_computation.12 | convolution fusion | flops 2148007936 | bytes 10485760 | tf_op jit(solution)/shard_map/dot_general | solution.py:325
  16.9 89.9 %ring_attention.1 = bf16[256,2048]{1,0:T(8,128)(2,1)S(1)} custom-call(bf16[256,2048]{1,0:T(8,128)(2,1)S(1)} %fusion.12.q_ref, bf16[2,2,128,128]{3,2,1,0:T(8,128)(2,1)S(1)} %fusion.31.kt_ref, bf16[2,2,128,128]{3,2,1,0:T(8,128)(2,1)S(1)} %fusion.32.v_ref), custom_call_target="tpu_custom_call" | custom-call | tf_op jit(solution)/shard_map/ring_attention/pallas_call | solution.py:281
  106.8 0.0 slice-done
  106.8 0.0 slice-done.1
  106.8 3.7 %fusion.47.p_ref = f32[256,2048]{1,0:T(8,128)} fusion(bf16[256,2048]{1,0:T(8,128)(2,1)S(1)} %ring_attention.1, bf16[2048,2048]{1,0:T(8,128)(2,1)S(1)} %bitcast.104), kind=kOutput, calls=%fused_computation.48 | convolution fusion | flops 2147483648 | bytes 11534336 | tf_op jit(solution)/shard_map/dot_general | solution.py:327
  110.5 5.3 %join_parts.1 = bf16[128,2048]{1,0:T(8,128)(2,1)} custom-call(f32[256,2048]{1,0:T(8,128)} %fusion.47.p_ref, bf16[128,2048]{1,0:T(8,128)(2,1)} %x_ref.3), custom_call_target="tpu_custom_call" | custom-call | tf_op jit(solution)/shard_map/join_parts/pallas_call | solution.py:59
  115.8 3.1 %fusion.48 = bf16[512,2048]{1,0:T(8,128)(2,1)} fusion(bf16[128,512]{1,0:T(8,128)(2,1)S(1)} %convert_reduce_fusion, bf16[128,2048]{1,0:T(8,128)(2,1)} %join_parts.1), kind=kOutput, calls=%fused_computation.49 | convolution fusion | flops 268435456 | bytes 2752512 | tf_op jit(solution)/shard_map/tkn,tm->nm/dot_general | solution.py:335
  118.9 4.1 %all_to_all.12 = bf16[128,4,2048]{2,1,0:T(4,128)(2,1)} reshape(bf16[512,2048]{1,0:T(8,128)(2,1)} %fusion.48) | data formatting | bytes 4194304 | tf_op jit(solution)/shard_map/all_to_all | solution.py:336
  123.0 0.0 copy-start.4
  123.0 39.7 %all_to_all.18 = bf16[128,4,2048]{2,1,0:T(4,128)(2,1)S(1)} all-to-all(bf16[128,4,2048]{2,1,0:T(4,128)(2,1)} %all_to_all.12), channel_id=1, replica_groups=mesh['data'=1,'cp'=64,'tp'=2] {'cp','tp'}, dimensions={0} | all-to-all | bytes 4194304 | tf_op jit(solution)/shard_map/all_to_all | solution.py:336
  162.7 0.0 copy-start.3
  162.7 1.3 copy-done.3
  164.0 0.0 copy-done.4
  164.0 4.8 %fusion.7 = f32[128,4,768]{2,0,1:T(8,128)} fusion(bf16[1,2048,768]{2,1,0:T(8,128)(2,1)S(1)} %copy-done.4, bf16[128,4,2048]{2,1,0:T(4,128)(2,1)S(1)} %all_to_all.18), kind=kOutput, calls=%fused_computation.7 | convolution fusion | flops 1610612736 | bytes 6815744 | tf_op jit(solution)/shard_map/secm,emf->secf/dot_general | solution.py:338
  168.8 0.0 copy-done
  168.8 9.8 %fusion.9 = bf16[128,4,2048]{2,0,1:T(8,128)(2,1)} fusion(bf16[1,768,2048]{2,1,0:T(8,128)(2,1)S(1)} %copy-done, bf16[1,2048,768]{2,1,0:T(8,128)(2,1)} %param.18, bf16[128,4,2048]{2,1,0:T(4,128)(2,1)} %copy-done.3, f32[128,4,768]{2,0,1:T(8,128)} %fusion.7), kind=kOutput, calls=%fused_computation.10 | convolution fusion | flops 3224633344 | bytes 12058624 | tf_op jit(solution)/shard_map/secf,efm->secm/dot_general | solution.py:341
  178.6 3.2 %copy.49 = bf16[128,4,2048]{2,1,0:T(4,128)(2,1)S(1)} copy(bf16[128,4,2048]{2,0,1:T(8,128)(2,1)} %fusion.9) | data formatting | bytes 4194304 | tf_op jit(solution)/shard_map/convert_element_type | solution.py:341
  181.8 37.0 %all_to_all.19 = bf16[128,4,2048]{2,1,0:T(4,128)(2,1)} all-to-all(bf16[128,4,2048]{2,1,0:T(4,128)(2,1)S(1)} %copy.49), channel_id=1, replica_groups=mesh['data'=1,'cp'=64,'tp'=2] {'cp','tp'}, dimensions={0} | all-to-all | bytes 4194304 | tf_op jit(solution)/shard_map/all_to_all | solution.py:342
  218.8 0.0 copy-start.7
  218.8 4.0 %reshape.83 = bf16[512,2048,1]{1,0,2:T(8,128)(2,1)} reshape(bf16[128,4,2048]{2,1,0:T(4,128)(2,1)} %all_to_all.19) | data formatting | bytes 4194304 | tf_op jit(solution)/shard_map/all_to_all | solution.py:342
  222.8 0.0 copy-done.7
  222.8 0.0 copy-start.1
  222.8 2.6 %fusion.21 = f32[128,2048]{1,0:T(8,128)S(1)} fusion(bf16[512,2048,1]{1,0,2:T(8,128)(2,1)} %reshape.83, f32[128,2]{0,1:T(2,128)S(1)} %copy-done.7, s32[128,2]{0,1:T(2,128)S(1)} %multiply_add_fusion), kind=kOutput, calls=%fused_computation.22 | convolution fusion | flops 537788416 | bytes 3147776 | tf_op jit(solution)/shard_map/tkn,nm->tkm/dot_general | solution.py:343
  225.4 0.0 copy-done.1
  225.4 0.9 add_convert_fusion
  (8 shorter events, 0.1 us)
Async XLA Ops:
  0.0 168.8 %copy-start = (bf16[1,768,2048]{2,1,0:T(8,128)(2,1)S(1)}, bf16[1,768,2048]{2,1,0:T(8,128)(2,1)}, u32[]{:S(2)}) copy-start(bf16[1,768,2048]{2,1,0:T(8,128)(2,1)} %param.19) | copy-start | bytes 9437188
  7.9 1.5 copy-start.5
  7.9 2.0 copy-start.6
  9.4 1.3 copy-start.2
  9.9 96.9 %slice-start = ((s8[8388608]{0:T(1024)(128)(4,1)}), s8[4194304]{0:T(1024)(128)(4,1)S(1)}, s32[]{:S(2)}) async-start(s8[8388608]{0:T(1024)(128)(4,1)} %bitcast.102), calls=%async_computation.2 | async-start | bytes 8388608
  10.7 96.1 %slice-start.1 = ((s8[8388608]{0:T(1024)(128)(4,1)}), s8[4194304]{0:T(1024)(128)(4,1)S(1)}, s32[]{:S(2)}) async-start(s8[8388608]{0:T(1024)(128)(4,1)} %bitcast.102), calls=%async_computation.3 | async-start | bytes 8388608
  123.0 41.0 %copy-start.4 = (bf16[1,2048,768]{2,1,0:T(8,128)(2,1)S(1)}, bf16[1,2048,768]{2,1,0:T(8,128)(2,1)}, u32[]{:S(2)}) copy-start(bf16[1,2048,768]{2,1,0:T(8,128)(2,1)} %param.17) | copy-start | bytes 9437188
  162.7 1.4 copy-start.3
  218.8 4.0 %copy-start.7 = (f32[128,2]{0,1:T(2,128)S(1)}, f32[128,2]{0,1:T(2,128)}, u32[]{:S(2)}) copy-start(f32[128,2]{0,1:T(2,128)} %param.16) | copy-start | bytes 3076
  222.8 2.6 %copy-start.1 = (bf16[128,2048]{1,0:T(8,128)(2,1)S(1)}, bf16[128,2048]{1,0:T(8,128)(2,1)}, u32[]{:S(2)}) copy-start(bf16[128,2048]{1,0:T(8,128)(2,1)} %join_parts.1) | copy-start | bytes 1572868

commit v2 on v1

--- a/solution.py
+++ b/solution.py
@@ -302,6 +302,124 @@
     )(q, kt, val)
 
 
+def moe_kernel(h_ref, st_ref, s_ref, g_ref, wg_hbm, wu_hbm, wd_hbm, y_ref, send, recv, res, back, wg, wu, wd, w_sem, hop, s_ss, s_rs, r_ss, r_rs):
+    cp, tp = lax.axis_index('cp'), lax.axis_index('tp')
+    me = cp * 2 + tp
+    x, y, z = cp % 4, (cp // 4) % 4, cp // 16
+    n_dev, cap, width = send.shape
+    n_grp = s_rs.shape[0]
+    per = n_dev // n_grp
+    rows = per * cap
+
+    def dev(xx, yy, zz, t):
+        return (0, (zz % 4) * 16 + (yy % 4) * 4 + xx % 4, t)
+
+    loads = [pltpu.make_async_copy(a, b, w_sem.at[i]) for i, (a, b) in enumerate(((wg_hbm, wg), (wu_hbm, wu), (wd_hbm, wd)))]
+    for copy in loads:
+        copy.start()
+    barrier = pltpu.get_barrier_semaphore()
+    for d in STEPS:
+        pl.semaphore_signal(barrier, inc=1, device_id=dev(x + d, y, z, tp), device_id_type=MESH)
+        pl.semaphore_signal(barrier, inc=1, device_id=dev(x, y + d, z, tp), device_id_type=MESH)
+        pl.semaphore_signal(barrier, inc=1, device_id=dev(x, y, z + d, tp), device_id_type=MESH)
+    pl.semaphore_signal(barrier, inc=1, device_id=dev(x, y, z, 1 - tp), device_id_type=MESH)
+
+    def pack(lo):
+        at = lax.broadcasted_iota(jnp.int32, (rows, st_ref.shape[1]), 0) + lo * rows
+        pick = (at == st_ref[0:1, :]) | (at == st_ref[1:2, :])
+        out = jnp.dot(pick.astype(jnp.bfloat16), h_ref[...], preferred_element_type=jnp.float32)
+        send[pl.ds(lo * per, per)] = out.astype(jnp.bfloat16).reshape(per, cap, width)
+
+    for lo in range(n_grp):
+        pack(lo)
+
+    pl.semaphore_wait(barrier, 10)
+    for d in STEPS:
+        pl.semaphore_signal(hop.at[0], inc=1, device_id=dev(x, y + d, z, tp), device_id_type=MESH)
+    pl.semaphore_wait(hop.at[0], 3)
+    for d in STEPS:
+        pl.semaphore_signal(hop.at[1], inc=1, device_id=dev(x, y, z + d, tp), device_id_type=MESH)
+    pl.semaphore_wait(hop.at[1], 3)
+    pl.semaphore_signal(hop.at[2], inc=1, device_id=dev(x, y, z, 1 - tp), device_id_type=MESH)
+    pl.semaphore_wait(hop.at[2], 1)
+
+    def peer(k, sign):
+        j = (k * 91) % n_dev
+        xx = (x + sign * ((j // 2) % 4)) % 4
+        yy = (y + sign * ((j // 8) % 4)) % 4
+        zz = (z + sign * (j // 32)) % 4
+        return zz * 16 + yy * 4 + xx, (tp + j) % 2
+
+    def give(k, _):
+        c, t = peer(k, 1)
+        pltpu.make_async_remote_copy(src_ref=send.at[c * 2 + t], dst_ref=recv.at[k], send_sem=s_ss, recv_sem=s_rs.at[k // per], device_id=(0, c, t), device_id_type=MESH).start()
+        return 0
+
+    own = pltpu.make_async_copy(send.at[me], recv.at[0], s_rs.at[0])
+    own.start()
+    lax.fori_loop(1, n_dev, give, 0)
+    for copy in loads:
+        copy.wait()
+
+    def answer(k, _):
+        c, t = peer(k, 3)
+        pltpu.make_async_remote_copy(src_ref=res.at[k], dst_ref=back.at[me], send_sem=r_ss, recv_sem=r_rs, device_id=(0, c, t), device_id_type=MESH).start()
+        return 0
+
+    def group(i, _):
+        part = recv.at[pl.ds(i * per, per)]
+        pltpu.make_async_copy(part, part, s_rs.at[i]).wait()
+        rows_in = part[...].reshape(rows, width)
+        gate = jnp.dot(rows_in, wg[...], preferred_element_type=jnp.float32)
+        up = jnp.dot(rows_in, wu[...], preferred_element_type=jnp.float32)
+        act = (jax.nn.silu(gate) * up).astype(jnp.bfloat16)
+        out = jnp.dot(act, wd[...], preferred_element_type=jnp.float32)
+        res[pl.ds(i * per, per)] = out.astype(jnp.bfloat16).reshape(per, cap, width)
+        lax.fori_loop(jnp.maximum(i * per, 1), (i + 1) * per, answer, 0)
+        return 0
+
+    lax.fori_loop(0, n_grp, group, 0)
+    own_back = pltpu.make_async_copy(res.at[0], back.at[me], r_rs)
+    own_back.start()
+    pltpu.make_async_copy(back, back, r_rs).wait()
+    all_back = back[...].reshape(n_dev * cap, width)
+    at = lax.broadcasted_iota(jnp.int32, (s_ref.shape[0], n_dev * cap), 1)
+    total = h_ref[...].astype(jnp.float32)
+    moe = None
+    for j in range(2):
+        pick = (at == s_ref[:, j:j + 1]).astype(jnp.bfloat16)
+        term = g_ref[:, j:j + 1] * jnp.dot(pick, all_back, preferred_element_type=jnp.float32)
+        moe = term if moe is None else moe + term
+    y_ref[...] = (total + moe).astype(y_ref.dtype)
+    most = send.at[pl.ds(1, n_dev - 1)]
+    pltpu.make_async_copy(most, most, s_ss).wait()
+    pltpu.make_async_copy(most, most, r_ss).wait()
+
+
+def moe(hidden, slot_ids, gates, w_gate, w_up, w_down, cap):
+    d_model, ff = w_gate.shape
+    n_dev = 4 * hidden.shape[0] // cap
+    dma = pltpu.SemaphoreType.DMA
+    bf = jnp.bfloat16
+    vm = pl.BlockSpec(memory_space=pltpu.VMEM)
+    anyspace = pl.BlockSpec(memory_space=pl.ANY)
+    buf = pltpu.VMEM((n_dev, cap, d_model), bf)
+    n_grp = 4
+    return pl.pallas_call(
+        moe_kernel,
+        out_shape=jax.ShapeDtypeStruct(hidden.shape, bf),
+        in_specs=[vm] * 4 + [anyspace] * 3,
+        out_specs=vm,
+        scratch_shapes=[
+            buf, buf, buf, buf,
+            pltpu.VMEM((d_model, ff), bf), pltpu.VMEM((d_model, ff), bf), pltpu.VMEM((ff, d_model), bf),
+            dma((3,)), pltpu.SemaphoreType.REGULAR((3,)), dma, dma((n_grp,)), dma, dma,
+        ],
+        compiler_params=pltpu.CompilerParams(collective_id=4, has_side_effects=True, vmem_limit_bytes=48 * 1024 * 1024),
+        name='moe_exchange',
+    )(hidden, slot_ids.T, slot_ids, gates, w_gate, w_up, w_down)
+
+
 def solution(mesh):
     cp_size = mesh.shape['cp']
     tp_size = mesh.shape['tp']
@@ -331,17 +449,6 @@
         onehot = (flat_ids[:, None] == jnp.arange(num_exp)[None, :]).astype(jnp.int32)
         slot_pos = jnp.sum(jnp.cumsum(onehot, axis=0) * onehot, axis=1) - 1
         slot_ids = (flat_ids * capacity + slot_pos).reshape(tok_dev, 2)
-        select = (slot_ids[:, :, None] == jnp.arange(num_exp * capacity)[None, None, :]).astype(jnp.bfloat16)
-        send_buf = jnp.einsum('tkn,tm->nm', select, hidden, preferred_element_type=jnp.float32).astype(jnp.bfloat16)
-        recv_buf = lax.all_to_all(send_buf, ('cp', 'tp'), 0, 0, tiled=True)
-        tok_in = recv_buf.reshape(num_devs, exp_local, capacity, -1)
-        gate_pre = jnp.einsum('secm,emf->secf', tok_in, w_gate, preferred_element_type=jnp.float32)
-        up_pre = jnp.einsum('secm,emf->secf', tok_in, w_up, preferred_element_type=jnp.float32)
-        hid_act = (jax.nn.silu(gate_pre) * up_pre).astype(jnp.bfloat16)
-        exp_out = jnp.einsum('secf,efm->secm', hid_act, w_down, preferred_element_type=jnp.float32).astype(jnp.bfloat16)
-        back_buf = lax.all_to_all(exp_out.reshape(num_devs * exp_local * capacity, -1), ('cp', 'tp'), 0, 0, tiled=True)
-        picked = jnp.einsum('tkn,nm->tkm', select, back_buf, preferred_element_type=jnp.float32)
-        moe_out = jnp.sum(gate_blk[:, :, None] * picked, axis=1)
-        return (hidden.astype(jnp.float32) + moe_out).astype(jnp.bfloat16)
+        return moe(hidden, slot_ids, gate_blk, w_gate[0], w_up[0], w_down[0], capacity)
 
     return jax.shard_map(device_fn, mesh=mesh, in_specs=(row_spec, head_spec, head_spec, head_spec, wo_spec, row_spec, row_spec, expert_spec, expert_spec, expert_spec), out_specs=row_spec, check_vma=False)

time: 227 us -> 181 us (0.80)
  blocking collectives: 76.7 us -> 0 us
  Pallas kernels: 100 us -> 164 us
  matrix products: 31.1 us -> 10.9 us
  local copies, waits for them, and re-layouts: 16 us -> 4.82 us
    all_to_all x2 -> x0, blocking collectives: 76.7 us -> none  [the longest x1 39.7 us: device_fn(): recv_buf = lax.all_to_all(send_buf, ('cp', 'tp'), 0, 0, tiled=True)]
    pallas_call x0 -> x1, Pallas kernels: none -> 64 us  [moe(): pl.pallas_call(moe_kernel, out_shape=jax.ShapeDtypeStruct(hidden.shape, b...]
    dot_general x4 -> x0, matrix products: 20.2 us -> none  [the longest x1 9.8 us: device_fn(): jnp.einsum('secf,efm->secm', hid_act, w_down, preferred_element_type=jnp....]
    all_to_all x2 -> x0, local copies, waits for them, and re-layouts: 8.1 us -> none  [the longest x1 4.12 us: device_fn(): recv_buf = lax.all_to_all(send_buf, ('cp', 'tp'), 0, 0, tiled=True)]
    convert_element_type x1 -> x0, local copies, waits for them, and re-layouts: 3.21 us -> none  [device_fn(): jnp.einsum('secf,efm->secm', hid_act, w_down, preferred_element_type=jnp....]
where the time goes in v2:
time: 181 us
  Pallas kernels  164 us (91%)
  matrix products  10.9 us (6%)
  local copies, waits for them, and re-layouts  4.82 us (3%)
    pallas_call x1, Pallas kernels, attention(): pl.pallas_call(functools.partial(attn_kernel, 128 ** (-0.5) * math.log2(m...  90 us
    pallas_call x1, Pallas kernels, moe(): pl.pallas_call(moe_kernel, out_shape=jax.ShapeDtypeStruct(hidden.shape, b...  64 us
    dot_general x1, matrix products, device_fn(): jnp.dot(x_rows, w_q.reshape(d_model, -1), preferred_element_type=jnp.floa...  6.19 us
    pallas_call x1, Pallas kernels, join_parts(): pl.pallas_call(join_kernel, out_shape=jax.ShapeDtypeStruct(x.shape, x.dty...  5.27 us
    pallas_call x1, Pallas kernels, swap_rows(): pl.pallas_call(swap_kernel, out_shape=jax.ShapeDtypeStruct((2 * rows, col...  5.07 us
    unnamed x20, local copies, waits for them, and re-layouts  4 us
    dot_general x1, matrix products, device_fn(): jnp.dot(head_out, w_o.reshape(-1, d_model), preferred_element_type=jnp.fl...  3.68 us

profile of v2, /device:TPU:1, one launch (start us, length us, event | category | flops | bytes accessed | tf_op | source)
XLA Modules:
  0.0 180.6 jit_solution(9242230090018654628)
XLA Ops:
  0.0 0.0 copy-start
  0.0 5.1 %swap_rows.1 = bf16[256,2048]{1,0:T(8,128)(2,1)} custom-call(bf16[128,2048]{1,0:T(8,128)(2,1)} %x_ref.3), custom_call_target="tpu_custom_call" | custom-call | tf_op jit(solution)/shard_map/swap_rows/pallas_call | solution.py:32
  5.1 0.0 copy-start.3
  5.1 0.0 copy-start.7
  5.1 6.2 %fusion.3.q_ref = bf16[256,2048]{1,0:T(8,128)(2,1)S(1)} fusion(bf16[256,2048]{1,0:T(8,128)(2,1)} %swap_rows.1, bf16[256,8,16,128]{3,2,1,0:T(8,128)(2,1)} %bitcast.50), kind=kOutput, calls=%fused_computation.3 | convolution fusion | flops 2148007936 | bytes 10485760 | tf_op jit(solution)/shard_map/dot_general | solution.py:443
  11.3 0.0 copy-start.6
  11.3 0.0 copy-done.3
  11.3 0.1 copy.24
  11.4 0.0 copy-done
  11.4 0.6 fusion.6.kt_ref
  12.0 0.0 copy-done.7
  12.0 0.4 fusion.7.v_ref
  12.5 90.0 %ring_attention.1 = bf16[256,2048]{1,0:T(8,128)(2,1)S(1)} custom-call(bf16[256,2048]{1,0:T(8,128)(2,1)S(1)} %fusion.3.q_ref, bf16[2,2,128,128]{3,2,1,0:T(8,128)(2,1)S(1)} %fusion.6.kt_ref, bf16[2,2,128,128]{3,2,1,0:T(8,128)(2,1)S(1)} %fusion.7.v_ref), custom_call_target="tpu_custom_call" | custom-call | tf_op jit(solution)/shard_map/ring_attention/pallas_call | solution.py:281
  102.4 0.0 copy-done.6
  102.4 0.0 copy-start.4
  102.5 0.0 copy-start.5
  102.5 3.7 %fusion.14.p_ref = f32[256,2048]{1,0:T(8,128)} fusion(bf16[256,2048]{1,0:T(8,128)(2,1)S(1)} %ring_attention.1, bf16[2048,2048]{1,0:T(8,128)(2,1)S(1)} %bitcast.51), kind=kOutput, calls=%fused_computation.21 | convolution fusion | flops 2147483648 | bytes 11534336 | tf_op jit(solution)/shard_map/dot_general | solution.py:445
  106.2 5.3 %join_parts.1.h_ref = bf16[128,2048]{1,0:T(8,128)(2,1)} custom-call(f32[256,2048]{1,0:T(8,128)} %fusion.14.p_ref, bf16[128,2048]{1,0:T(8,128)(2,1)} %x_ref.3), custom_call_target="tpu_custom_call" | custom-call | tf_op jit(solution)/shard_map/join_parts/pallas_call | solution.py:59
  111.4 0.0 copy-done.4
  111.4 0.1 copy.33
  111.6 0.1 copy.29
  111.7 0.1 eq.29
  111.8 0.1 copy.31
  111.9 0.2 fusion.10
  112.2 0.1 eq.25
  112.4 0.2 fusion.11
  112.6 0.1 sub.7
  112.7 0.1 copy.34.st_ref
  112.8 0.0 copy-done.5
  112.8 0.1 copy.35.g_ref
  112.9 0.0 copy-start.1
  112.9 1.9 %copy-done.1 = bf16[1,2048,768]{2,1,0:T(8,128)(2,1)S(1)} copy-done((bf16[1,2048,768]{2,1,0:T(8,128)(2,1)S(1)}, bf16[1,2048,768]{2,1,0:T(8,128)(2,1)}, u32[]{:S(2)}) %copy-start.1) | copy-done | bytes 3145752
  114.8 0.0 copy-start.2
  114.8 1.0 copy-done.2
  115.9 64.0 %moe_exchange.1 = bf16[128,2048]{1,0:T(8,128)(2,1)S(1)} custom-call(bf16[128,2048]{1,0:T(8,128)(2,1)S(1)} %copy-done.2, s32[2,128]{1,0:T(2,128)S(1)} %copy.34.st_ref, s32[128,2]{1,0:T(8,128)S(1)} %add.7.s_ref, f32[128,2]{1,0:T(8,128)S(1)} %copy.35.g_ref, bf16[2048,768]{1,0:T(8,128)(2,1)S(1)} %bitcast.40, bf16[2048,768]{1,0:T(8,128)(2,1)} %bitcast.43, ...), custom_call_target="tpu_custom_call" | custom-call | tf_op jit(solution)/shard_map/moe_exchange/pallas_call | solution.py:408
  179.8 0.8 copy.56
  (9 shorter events, 0.1 us)
Async XLA Ops:
  0.0 11.4 %copy-start = (bf16[2048,2,128]{2,1,0:T(2,128)(2,1)S(1)}, bf16[2048,2,128]{2,1,0:T(2,128)(2,1)}, u32[]{:S(2)}) copy-start(bf16[2048,2,128]{2,1,0:T(2,128)(2,1)} %param.12) | copy-start | bytes 3145732
  5.1 6.2 %copy-start.3 = (bf16[256,2048]{1,0:T(8,128)(2,1)S(1)}, bf16[256,2048]{1,0:T(8,128)(2,1)}, u32[]{:S(2)}) copy-start(bf16[256,2048]{1,0:T(8,128)(2,1)} %swap_rows.1) | copy-start | bytes 3145732
  5.1 6.9 %copy-start.7 = (bf16[2048,2,128]{2,1,0:T(2,128)(2,1)S(1)}, bf16[2048,2,128]{2,1,0:T(2,128)(2,1)}, u32[]{:S(2)}) copy-start(bf16[2048,2,128]{2,1,0:T(2,128)(2,1)} %param.13) | copy-start | bytes 3145732
  11.3 91.1 %copy-start.6 = (bf16[16,128,2048]{2,1,0:T(8,128)(2,1)S(1)}, bf16[16,128,2048]{2,1,0:T(8,128)(2,1)}, u32[]{:S(2)}) copy-start(bf16[16,128,2048]{2,1,0:T(8,128)(2,1)} %param.14) | copy-start | bytes 25165828
  102.4 9.0 %copy-start.4 = (s32[128,2]{0,1:T(2,128)S(1)}, s32[128,2]{0,1:T(2,128)}, u32[]{:S(2)}) copy-start(s32[128,2]{0,1:T(2,128)} %param.15) | copy-start | bytes 3076
  102.5 10.3 %copy-start.5 = (f32[128,2]{0,1:T(2,128)S(1)}, f32[128,2]{0,1:T(2,128)}, u32[]{:S(2)}) copy-start(f32[128,2]{0,1:T(2,128)} %param.16) | copy-start | bytes 3076
  112.9 1.9 %copy-start.1 = (bf16[1,2048,768]{2,1,0:T(8,128)(2,1)S(1)}, bf16[1,2048,768]{2,1,0:T(8,128)(2,1)}, u32[]{:S(2)}) copy-start(bf16[1,2048,768]{2,1,0:T(8,128)(2,1)} %param.17) | copy-start | bytes 9437188
  114.8 1.0 copy-start.2

commit v3 on v2

--- a/solution.py
+++ b/solution.py
@@ -40,46 +40,18 @@
     )(x)
 
 
-def join_kernel(p_ref, x_ref, o_ref, buf, ssem, rsem):
-    cp, tp = lax.axis_index('cp'), lax.axis_index('tp')
-    peer = (0, cp, 1 - tp)
-    rows = x_ref.shape[0]
-    barrier = pltpu.get_barrier_semaphore()
-    pl.semaphore_signal(barrier, inc=1, device_id=peer, device_id_type=MESH)
-    pl.semaphore_wait(barrier, 1)
-    away = p_ref.at[pl.ds(pl.multiple_of((1 - tp) * rows, rows), rows)]
-    copy = pltpu.make_async_remote_copy(src_ref=away, dst_ref=buf, send_sem=ssem, recv_sem=rsem, device_id=peer, device_id_type=MESH)
-    copy.start()
-    copy.wait()
-    mine = p_ref[pl.ds(pl.multiple_of(tp * rows, rows), rows), :]
-    o_ref[...] = (x_ref[...].astype(jnp.float32) + (mine + buf[...])).astype(o_ref.dtype)
-
-
-def join_parts(part, x):
-    return pl.pallas_call(
-        join_kernel,
-        out_shape=jax.ShapeDtypeStruct(x.shape, x.dtype),
-        in_specs=[pl.BlockSpec(memory_space=pltpu.VMEM)] * 2,
-        out_specs=pl.BlockSpec(memory_space=pltpu.VMEM),
-        scratch_shapes=[pltpu.VMEM(x.shape, jnp.float32), pltpu.SemaphoreType.DMA, pltpu.SemaphoreType.DMA],
-        compiler_params=pltpu.CompilerParams(collective_id=2, has_side_effects=True),
-        name='join_parts',
-    )(part, x)
-
-
 def ring_step(i):
     return 1 + 2 * i - 3 * (i // 2)
 
 
-def attn_kernel(scale2, q_ref, kt_ref, v_ref, o_ref, qb, kb, vb, so, ob, acc_s, m_s, l_s,
-                q_ss, k_ss, v_ss, o_ss, q_rs, kx_rs, vx_rs, o_rs, k_rs, v_rs, kp_rs, vp_rs, kd_ss, vd_ss, kf_ss, vf_ss, kp_ss, vp_ss):
+def attn_kernel(scale2, q_ref, kt_ref, v_ref, x_ref, wo_hbm, h_ref, qb, kb, vb, so, ob, wo, part, jb, acc_s, m_s, l_s,
+                wo_sem, q_ss, k_ss, v_ss, o_ss, q_rs, kx_rs, vx_rs, o_rs, k_rs, v_rs, kp_rs, vp_rs, kd_ss, vd_ss, kf_ss, vf_ss, kp_ss, vp_ss, j_ss, j_rs):
     cp, c = lax.axis_index('cp'), lax.axis_index('tp')
     x, y, z = cp % 4, (cp // 4) % 4, cp // 16
     g = z * 4 + y
     seg = kt_ref.shape[-1]
     half = seg // 2
-    wide = so.shape[-1]
-    heads = wide // 128
+    heads = qb.shape[0]
 
     def dev(xx, yy, zz, t):
         return (0, (zz % 4) * 16 + (yy % 4) * 4 + xx % 4, t)
@@ -91,6 +63,9 @@
         pl.semaphore_signal(barrier, inc=1, device_id=dev(x, y + d, z, c), device_id_type=MESH)
         pl.semaphore_signal(barrier, inc=1, device_id=dev(x, y, z + d, c), device_id_type=MESH)
     pl.semaphore_signal(barrier, inc=1, device_id=dev(x, y, z, 1 - c), device_id_type=MESH)
+    wo_loads = [pltpu.make_async_copy(wo_hbm.at[:, hh], wo.at[hh], wo_sem.at[hh]) for hh in range(heads)]
+    for copy in wo_loads:
+        copy.start()
     pl.semaphore_wait(barrier, 13)
 
     def move(src, dst, ssem, rsem, xx, t, start):
@@ -115,10 +90,11 @@
                 i = j * 2 + t
                 move(kt_ref.at[j, t], kb.at[t, g, x], k_ss.at[i], kx_rs, 2 * c + j, t, start)
                 move(v_ref.at[j, t], vb.at[t, g, x], v_ss.at[i], vx_rs, 2 * c + j, t, start)
-        for j in range(2):
-            for t in range(2):
-                i = j * 2 + t
-                move(q_ref.at[:, pl.ds(i * wide, wide)], qb.at[x], q_ss.at[i], q_rs, 2 * c + j, t, start)
+        for hh in range(heads):
+            for j in range(2):
+                for t in range(2):
+                    i = j * 2 + t
+                    move(q_ref.at[:, pl.ds((i * heads + hh) * 128, 128)], qb.at[hh, x], q_ss.at[hh, i], q_rs.at[hh], 2 * c + j, t, start)
 
     def arrived(ref, sem):
         pltpu.make_async_copy(ref, ref, sem).wait()
@@ -129,6 +105,21 @@
     def to_partner(gg):
         push(kb, gg, y, z, 1 - c, kp_ss, kp_rs)
         push(vb, gg, y, z, 1 - c, vp_ss, vp_rs)
+
+    def group(dy, dz):
+        return ((z + 4 - dz) % 4) * 4 + (y + 4 - dy) % 4
+
+    def pass_direct(i):
+        d = ring_step(i)
+        gy, gz = group(d, 0), group(0, d)
+        for gg in (gy, gz):
+            arrived(kb.at[c, gg], k_rs.at[gg])
+            arrived(vb.at[c, gg], v_rs.at[gg])
+        for e in STEPS:
+            push(kb, gy, y, z + e, c, kf_ss, k_rs)
+            push(vb, gz, y + e, z, c, vf_ss, v_rs)
+        to_partner(gy)
+        to_partner(gz)
 
     exchange(True)
     arrived(kb.at[c, g], kx_rs)
@@ -140,28 +131,22 @@
         push(vb, g, y, z + d, c, vd_ss, v_rs)
         if d == 1:
             to_partner(g)
-    arrived(qb, q_rs)
-
-    units = [(hh, xp) for hh in range(heads) for xp in range(2)]
+
     keys = 4 * seg
     rows = 2 * seg
 
     def q_unit(qs, hh, xp):
-        parts = [qb[xx, pl.ds(pl.multiple_of(t * seg + qs * half, half), half), hh * 128:(hh + 1) * 128] for xx in (2 * xp, 2 * xp + 1) for t in range(2)]
+        parts = [qb[hh, xx, pl.ds(pl.multiple_of(t * seg + qs * half, half), half), :] for xx in (2 * xp, 2 * xp + 1) for t in range(2)]
         return jnp.concatenate(parts, axis=0)
 
-    def tiles(gg, work):
-        todo = []
-        for qs, h, masked, first in work:
+    def tiles(todo):
+        def score(item):
+            gg, qs, h, masked, first, hh, xp = item
             kt = jnp.concatenate([kb[h, gg, i] for i in range(4)], axis=1)
-            todo += [(qs, h, masked, first, kt, hh, xp) for hh, xp in units]
-
-        def score(item):
-            qs, h, masked, first, kt, hh, xp = item
             return jnp.dot(q_unit(qs, hh, xp), kt, preferred_element_type=jnp.float32)
 
         s_next = score(todo[0])
-        for n, (qs, h, masked, first, kt, hh, xp) in enumerate(todo):
+        for n, (gg, qs, h, masked, first, hh, xp) in enumerate(todo):
             s = s_next
             if n + 1 < len(todo):
                 s_next = score(todo[n + 1])
@@ -181,8 +166,7 @@
             ps = [jnp.exp2(s[:, i * 128:(i + 1) * 128] * scale2 - m_new) for i in range(4)]
             lp = (ps[0] + ps[1]) + (ps[2] + ps[3])
             p = jnp.concatenate([v.astype(jnp.bfloat16) for v in ps], axis=1)
-            val = vb[h, gg].reshape(keys, 128)
-            pv = jnp.dot(p, val, preferred_element_type=jnp.float32)
+            pv = jnp.dot(p, vb[h, gg].reshape(keys, 128), preferred_element_type=jnp.float32)
             if first:
                 l_s[qs, hh, at] = lp
                 acc_s[qs, hh, at] = pv
@@ -194,39 +178,9 @@
         arrived(kb.at[1 - c, gg], kp_rs.at[gg])
         arrived(vb.at[1 - c, gg], vp_rs.at[gg])
 
-    def later(gg):
-        ready(gg)
+    def later(gg, hh):
         h = (gg > g).astype(jnp.int32)
-        tiles(gg, [(1, 0, False, False), (h, h, False, False)])
-
-    ready(g)
-    tiles(g, [(1, 0, False, True), (0, 0, True, True), (1, 1, True, False)])
-
-    def group(dy, dz):
-        return ((z + 4 - dz) % 4) * 4 + (y + 4 - dy) % 4
-
-    def pass_direct(i):
-        d = ring_step(i)
-        gy, gz = group(d, 0), group(0, d)
-        for gg in (gy, gz):
-            arrived(kb.at[c, gg], k_rs.at[gg])
-            arrived(vb.at[c, gg], v_rs.at[gg])
-            to_partner(gg)
-        for e in STEPS:
-            push(kb, gy, y, z + e, c, kf_ss, k_rs)
-            push(vb, gz, y + e, z, c, vf_ss, v_rs)
-
-    def direct(i, _):
-        @pl.when(i < 2)
-        def _():
-            pass_direct(i + 1)
-        d = ring_step(i)
-        later(group(d, 0))
-        later(group(0, d))
-        return 0
-
-    pass_direct(0)
-    lax.fori_loop(0, 3, direct, 0)
+        return [(gg, qs, hf, False, False, hh, xp) for qs, hf in ((1, 0), (h, h)) for xp in range(2)]
 
     def corner(i):
         return group(ring_step(i // 3), ring_step(i % 3))
@@ -237,33 +191,101 @@
         arrived(vb.at[c, gg], v_rs.at[gg])
         to_partner(gg)
 
-    def corners(i, _):
-        @pl.when(i < 8)
+    pass_direct(0)
+    ready(g)
+    near = [group(1, 0), group(0, 1), group(3, 0), group(0, 3)]
+
+    def first_phase(hh, _):
+        arrived(qb.at[hh], q_rs.at[hh])
+        tiles([(g, qs, hf, masked, first, hh, xp) for qs, hf, masked, first in ((1, 0, False, True), (0, 0, True, True), (1, 1, True, False)) for xp in range(2)])
+
+        @pl.when(hh == 0)
         def _():
-            pass_corner(i + 1)
-        later(corner(i))
-        return 0
-
+            pass_direct(1)
+            for gg in near:
+                ready(gg)
+
+        @pl.when(hh == 1)
+        def _():
+            pass_direct(2)
+
+        tiles([u for gg in near for u in later(gg, hh)])
+        return 0
+
+    lax.fori_loop(0, heads, first_phase, 0)
+
+    for gg in (group(2, 0), group(0, 2)):
+        ready(gg)
     pass_corner(0)
-    lax.fori_loop(0, 9, corners, 0)
-
-    for qs in range(2):
-        for hh, xp in units:
-            at = pl.ds(xp * rows, rows)
-            out = (acc_s[qs, hh, at] / jnp.sum(l_s[qs, hh, at], axis=1, keepdims=True)).astype(so.dtype)
-            for n, (xx, t) in enumerate([(xx, t) for xx in (2 * xp, 2 * xp + 1) for t in range(2)]):
-                so[xx, t * seg + qs * half:t * seg + (qs + 1) * half, hh * 128:(hh + 1) * 128] = out[n * half:(n + 1) * half]
-
-    def give_back(start):
+
+    def second_phase(i, _):
+        gg_far = corner(jnp.maximum(i - 2, 0))
+        gg = jnp.where(i == 0, group(2, 0), jnp.where(i == 1, group(0, 2), gg_far))
+
+        @pl.when(i >= 1)
+        def _():
+            pass_corner(i)
+
+        @pl.when(i >= 2)
+        def _():
+            ready(gg)
+
+        tiles([u for hh in range(heads) for u in later(gg, hh)])
+        return 0
+
+    lax.fori_loop(0, 7, second_phase, 0)
+
+    pass_corner(7)
+    pass_corner(8)
+    last = [corner(i) for i in range(5, 9)]
+    for gg in last:
+        ready(gg)
+
+    def o_move(hh, start):
         for i in range(4):
-            cols = pl.ds(pl.multiple_of(((x % 2) * 2 + c) * wide, wide), wide)
-            move(so.at[i], ob.at[:, cols], o_ss.at[i], o_rs, i, x // 2, start)
-
-    give_back(True)
-    arrived(ob, o_rs)
-    o_ref[...] = ob[...]
-    give_back(False)
+            move(so.at[hh, i], ob.at[hh, (x % 2) * 2 + c], o_ss.at[hh, i], o_rs.at[hh], i, x // 2, start)
+
+    def third_phase(hh, _):
+        tiles([u for gg in last for u in later(gg, hh)])
+        for qs in range(2):
+            for xp in range(2):
+                at = pl.ds(xp * rows, rows)
+                out = (acc_s[qs, hh, at] / jnp.sum(l_s[qs, hh, at], axis=1, keepdims=True)).astype(so.dtype)
+                for n, (xx, t) in enumerate([(xx, t) for xx in (2 * xp, 2 * xp + 1) for t in range(2)]):
+                    so[hh, xx, t * seg + qs * half:t * seg + (qs + 1) * half, :] = out[n * half:(n + 1) * half]
+        o_move(hh, True)
+        return 0
+
+    lax.fori_loop(0, heads, third_phase, 0)
+
+    n_blk = 4
+    wide = part.shape[1] // n_blk
+    away = pl.ds(pl.multiple_of((1 - c) * seg, seg), seg)
+    home = pl.ds(pl.multiple_of(c * seg, seg), seg)
+
+    def cols(b):
+        return pl.ds(b * wide, wide)
+
+    def joined(b):
+        return pltpu.make_async_remote_copy(src_ref=part.at[away, cols(b)], dst_ref=jb.at[:, cols(b)], send_sem=j_ss.at[b], recv_sem=j_rs.at[b], device_id=dev(x, y, z, 1 - c), device_id_type=MESH)
+
+    for hh in range(heads):
+        wo_loads[hh].wait()
+        arrived(ob.at[hh], o_rs.at[hh])
+        o_rows = jnp.concatenate([ob[hh, i] for i in range(4)], axis=1)
+        for b in range(n_blk):
+            term = jnp.dot(o_rows, wo[hh, :, :, b * wide:(b + 1) * wide].reshape(4 * 128, wide), preferred_element_type=jnp.float32)
+            part[:, b * wide:(b + 1) * wide] = term if hh == 0 else part[:, b * wide:(b + 1) * wide] + term
+            if hh == heads - 1:
+                joined(b).start()
+    for b in range(n_blk):
+        joined(b).wait()
+        at = slice(b * wide, (b + 1) * wide)
+        h_ref[:, at] = (x_ref[:, at].astype(jnp.float32) + (part[home, at] + jb[:, at])).astype(h_ref.dtype)
+
     exchange(False)
+    for hh in range(heads):
+        o_move(hh, False)
     arrived(kb.at[0, pl.ds(0, 6)], kd_ss)
     arrived(vb.at[0, pl.ds(0, 6)], vd_ss)
     arrived(kb.at[0, pl.ds(0, 9)], kf_ss)
@@ -272,34 +294,39 @@
     arrived(vb.at[0], vp_ss)
 
 
-def attention(q, kt, val):
+def attention(q, kt, val, x_blk, w_o):
     rows, cols = q.shape
     seg = kt.shape[-1]
-    wide = cols // 4
+    heads = cols // 512
+    d_model = x_blk.shape[1]
     dma = pltpu.SemaphoreType.DMA
     bf, f32 = jnp.bfloat16, jnp.float32
+    vm = pl.BlockSpec(memory_space=pltpu.VMEM)
     return pl.pallas_call(
         functools.partial(attn_kernel, (128 ** -0.5) * math.log2(math.e)),
-        out_shape=jax.ShapeDtypeStruct((rows, cols), bf),
-        in_specs=[pl.BlockSpec(memory_space=pltpu.VMEM)] * 3,
-        out_specs=pl.BlockSpec(memory_space=pltpu.VMEM),
+        out_shape=jax.ShapeDtypeStruct(x_blk.shape, bf),
+        in_specs=[vm] * 4 + [pl.BlockSpec(memory_space=pltpu.HBM)],
+        out_specs=vm,
         scratch_shapes=[
-            pltpu.VMEM((4, rows, wide), bf),
+            pltpu.VMEM((heads, 4, rows, 128), bf),
             pltpu.VMEM((2, 16, 4, seg, 128), bf),
             pltpu.VMEM((2, 16, 4, seg, 128), bf),
-            pltpu.VMEM((4, rows, wide), bf),
-            pltpu.VMEM((rows, cols), bf),
-            pltpu.VMEM((2, wide // 128, 4 * seg, 128), f32),
-            pltpu.VMEM((2, wide // 128, 4 * seg, 128), f32),
-            pltpu.VMEM((2, wide // 128, 4 * seg, 128), f32),
-            dma((4,)), dma((4,)), dma((4,)), dma((4,)),
-            dma, dma, dma, dma,
+            pltpu.VMEM((heads, 4, rows, 128), bf),
+            pltpu.VMEM((heads, 4, rows, 128), bf),
+            pltpu.VMEM((heads, 4, 128, d_model), bf),
+            pltpu.VMEM((rows, d_model), f32),
+            pltpu.VMEM(x_blk.shape, f32),
+            pltpu.VMEM((2, heads, 4 * seg, 128), f32),
+            pltpu.VMEM((2, heads, 4 * seg, 128), f32),
+            pltpu.VMEM((2, heads, 4 * seg, 128), f32),
+            dma((heads,)), dma((heads, 4)), dma((4,)), dma((4,)), dma((heads, 4)),
+            dma((heads,)), dma, dma, dma((heads,)),
             dma((16,)), dma((16,)), dma((16,)), dma((16,)),
-            dma, dma, dma, dma, dma, dma,
+            dma, dma, dma, dma, dma, dma, dma((4,)), dma((4,)),
         ],
-        compiler_params=pltpu.CompilerParams(collective_id=3, has_side_effects=True, vmem_limit_bytes=48 * 1024 * 1024),
+        compiler_params=pltpu.CompilerParams(collective_id=3, has_side_effects=True, vmem_limit_bytes=56 * 1024 * 1024),
         name='ring_attention',
-    )(q, kt, val)
+    )(q, kt, val, x_blk, w_o.reshape(4, heads, 128, d_model))
 
 
 def moe_kernel(h_ref, st_ref, s_ref, g_ref, wg_hbm, wu_hbm, wd_hbm, y_ref, send, recv, res, back, wg, wu, wd, w_sem, hop, s_ss, s_rs, r_ss, r_rs):
@@ -402,7 +429,7 @@
     dma = pltpu.SemaphoreType.DMA
     bf = jnp.bfloat16
     vm = pl.BlockSpec(memory_space=pltpu.VMEM)
-    anyspace = pl.BlockSpec(memory_space=pl.ANY)
+    anyspace = pl.BlockSpec(memory_space=pltpu.HBM)
     buf = pltpu.VMEM((n_dev, cap, d_model), bf)
     n_grp = 4
     return pl.pallas_call(
@@ -441,9 +468,7 @@
         key_t = jnp.einsum('mnc,hsm->nhcs', w_k, x_seg, preferred_element_type=jnp.float32).astype(jnp.bfloat16)
         val = jnp.einsum('hsm,mnc->nhsc', x_seg, w_v, preferred_element_type=jnp.float32).astype(jnp.bfloat16)
         queries = jnp.dot(x_rows, w_q.reshape(d_model, -1), preferred_element_type=jnp.float32).astype(jnp.bfloat16)
-        head_out = attention(queries, key_t, val)
-        part_sum = jnp.dot(head_out, w_o.reshape(-1, d_model), preferred_element_type=jnp.float32)
-        hidden = join_parts(part_sum, x_blk)
+        hidden = attention(queries, key_t, val, x_blk, w_o)
 
         flat_ids = idx_blk.reshape(-1)
         onehot = (flat_ids[:, None] == jnp.arange(num_exp)[None, :]).astype(jnp.int32)

time: 181 us -> 178 us (0.983)
  Pallas kernels: 164 us -> 158 us
  local copies, waits for them, and re-layouts: 4.82 us -> 6.77 us
    pallas_call x1 -> x0, Pallas kernels: 5.27 us -> none  [join_parts(): pl.pallas_call(join_kernel, out_shape=jax.ShapeDtypeStruct(x.shape, x.dty...]
    dot_general x1 -> x0, matrix products: 3.68 us -> none  [device_fn(): jnp.dot(head_out, w_o.reshape(-1, d_model), preferred_element_type=jnp.fl...]
    pallas_call x1, Pallas kernels: 64 us -> 61.7 us  [moe(): pl.pallas_call(moe_kernel, out_shape=jax.ShapeDtypeStruct(hidden.shape, b...]
    dot_general x1, matrix products: 0.45 us -> 2.32 us  [device_fn(): jnp.einsum('hsm,mnc->nhsc', x_seg, w_v, preferred_element_type=jnp.float32)]
    unnamed x20 -> x12, local copies, waits for them, and re-layouts: 4 us -> 4.72 us
where the time goes in v3:
time: 178 us; the launch traced here: 177 us
  Pallas kernels  158 us (89%)
  matrix products  10.6 us (6%)
  local copies, waits for them, and re-layouts  6.77 us (4%)
    pallas_call x1, Pallas kernels, attention(): pl.pallas_call(functools.partial(attn_kernel, 128 ** (-0.5) * math.log2(m...  91.7 us
    pallas_call x1, Pallas kernels, moe(): pl.pallas_call(moe_kernel, out_shape=jax.ShapeDtypeStruct(hidden.shape, b...  61.7 us
    dot_general x1, matrix products, device_fn(): jnp.dot(x_rows, w_q.reshape(d_model, -1), preferred_element_type=jnp.floa...  7.07 us
    pallas_call x1, Pallas kernels, swap_rows(): pl.pallas_call(swap_kernel, out_shape=jax.ShapeDtypeStruct((2 * rows, col...  5.04 us
    unnamed x12, local copies, waits for them, and re-layouts  4.72 us

profile of v3, /device:TPU:1, one launch (start us, length us, event | category | flops | bytes accessed | tf_op | source)
XLA Modules:
  0.0 177.1 jit_solution(18038850028306249909)
XLA Ops:
  0.0 0.0 copy-start
  0.0 0.9 copy.38
  0.9 0.1 eq.29
  1.0 0.1 copy.40
  1.1 0.2 fusion.10
  1.4 0.1 eq.25
  1.6 0.2 fusion.11
  1.8 0.1 sub.7
  1.9 0.7 broadcast_multiply_fusion
  2.6 0.1 copy.42
  2.7 0.1 copy.43.st_ref
  2.8 5.0 %swap_rows.1 = bf16[256,2048]{1,0:T(8,128)(2,1)} custom-call(bf16[128,2048]{1,0:T(8,128)(2,1)} %x_ref.3), custom_call_target="tpu_custom_call" | custom-call | tf_op jit(solution)/shard_map/swap_rows/pallas_call | solution.py:32
  7.8 1.3 copy.33
  9.2 0.0 copy-done
  9.2 1.2 fusion.6.kt_ref
  10.4 2.3 %fusion.7.v_ref = bf16[2,2,128,128]{3,2,1,0:T(8,128)(2,1)} fusion(bf16[2,128,2048,1]{2,1,0,3:T(8,128)(2,1)S(1)} %bitcast.45, bf16[2048,2,128,1]{2,1,0,3:T(2,128)(2,1)} %bitcast.50), kind=kOutput, calls=%fused_computation.7 | convolution fusion | flops 268500992 | bytes 2228224 | tf_op jit(solution)/shard_map/hsm,mnc->nhsc/dot_general | solution.py:469
  12.7 7.1 %fusion.3.q_ref = bf16[256,2048]{1,0:T(8,128)(2,1)} fusion(bf16[256,2048]{1,0:T(8,128)(2,1)} %swap_rows.1, bf16[256,8,16,128]{3,2,1,0:T(8,128)(2,1)} %bitcast.49), kind=kOutput, calls=%fused_computation.3 | convolution fusion | flops 2148007936 | bytes 10485760 | tf_op jit(solution)/shard_map/dot_general | solution.py:470
  19.8 0.0 copy-start.3
  19.8 91.7 %ring_attention.1.h_ref = bf16[128,2048]{1,0:T(8,128)(2,1)} custom-call(bf16[256,2048]{1,0:T(8,128)(2,1)} %fusion.3.q_ref, bf16[2,2,128,128]{3,2,1,0:T(8,128)(2,1)} %fusion.6.kt_ref, bf16[2,2,128,128]{3,2,1,0:T(8,128)(2,1)} %fusion.7.v_ref, bf16[128,2048]{1,0:T(8,128)(2,1)} %x_ref.3, bf16[4,4,128,2048]{3,2,1,0:T(8,128)(2,1)} %bitcast.40), custom_call_target="tpu_custom_call" | custom-call | tf_op jit(solution)/shard_map/ring_attention/pallas_call | solution.py:305
  111.6 0.0 copy-done.3
  111.6 0.1 copy.44.g_ref
  111.7 0.0 copy-start.1
  111.7 1.9 %copy-done.1 = bf16[1,2048,768]{2,1,0:T(8,128)(2,1)S(1)} copy-done((bf16[1,2048,768]{2,1,0:T(8,128)(2,1)S(1)}, bf16[1,2048,768]{2,1,0:T(8,128)(2,1)}, u32[]{:S(2)}) %copy-start.1) | copy-done | bytes 3145752
  113.6 0.0 copy-start.2
  113.6 1.0 copy-done.2
  114.6 61.7 %moe_exchange.1 = bf16[128,2048]{1,0:T(8,128)(2,1)S(1)} custom-call(bf16[128,2048]{1,0:T(8,128)(2,1)S(1)} %copy-done.2, s32[2,128]{1,0:T(2,128)S(1)} %copy.43.st_ref, s32[128,2]{1,0:T(8,128)S(1)} %add.7.s_ref, f32[128,2]{1,0:T(8,128)S(1)} %copy.44.g_ref, bf16[2048,768]{1,0:T(8,128)(2,1)S(1)} %bitcast.38, bf16[2048,768]{1,0:T(8,128)(2,1)} %bitcast.42, ...), custom_call_target="tpu_custom_call" | custom-call | tf_op jit(solution)/shard_map/moe_exchange/pallas_call | solution.py:435
  176.3 0.8 copy.65
  (8 shorter events, 0.1 us)
Async XLA Ops:
  0.0 9.2 %copy-start = (bf16[2048,2,128]{2,1,0:T(2,128)(2,1)S(1)}, bf16[2048,2,128]{2,1,0:T(2,128)(2,1)}, u32[]{:S(2)}) copy-start(bf16[2048,2,128]{2,1,0:T(2,128)(2,1)} %param.12) | copy-start | bytes 3145732
  19.8 91.7 %copy-start.3 = (f32[128,2]{0,1:T(2,128)S(1)}, f32[128,2]{0,1:T(2,128)}, u32[]{:S(2)}) copy-start(f32[128,2]{0,1:T(2,128)} %param.16) | copy-start | bytes 3076
  111.7 1.9 %copy-start.1 = (bf16[1,2048,768]{2,1,0:T(8,128)(2,1)S(1)}, bf16[1,2048,768]{2,1,0:T(8,128)(2,1)}, u32[]{:S(2)}) copy-start(bf16[1,2048,768]{2,1,0:T(8,128)(2,1)} %param.17) | copy-start | bytes 9437188
  113.6 1.0 copy-start.2

commit v4 on v3

v4 whole, which is shorter than its diff:
```python
import functools
import math

import jax
import jax.numpy as jnp
from jax import lax
from jax.experimental import pallas as pl
from jax.experimental.pallas import tpu as pltpu
from jax.sharding import PartitionSpec as P

NEG = -1e30
MESH = pl.DeviceIdType.MESH
STEPS = (1, 3, 2)


def swap_kernel(x_ref, o_ref, buf, ssem, rsem):
    cp, tp = lax.axis_index('cp'), lax.axis_index('tp')
    peer = (0, cp, 1 - tp)
    rows = x_ref.shape[0]
    barrier = pltpu.get_barrier_semaphore()
    pl.semaphore_signal(barrier, inc=1, device_id=peer, device_id_type=MESH)
    pl.semaphore_wait(barrier, 1)
    copy = pltpu.make_async_remote_copy(src_ref=x_ref, dst_ref=buf, send_sem=ssem, recv_sem=rsem, device_id=peer, device_id_type=MESH)
    copy.start()
    half = rows // 2

    def put(src, t):
        for h in range(2):
            o_ref[pl.ds(pl.multiple_of(h * rows + t * half, half), half), :] = src[h * half:(h + 1) * half]

    put(x_ref, tp)
    copy.wait()
    put(buf, 1 - tp)


def swap_rows(x):
    rows, cols = x.shape
    return pl.pallas_call(
        swap_kernel,
        out_shape=jax.ShapeDtypeStruct((2 * rows, cols), x.dtype),
        in_specs=[pl.BlockSpec(memory_space=pltpu.VMEM)],
        out_specs=pl.BlockSpec(memory_space=pltpu.VMEM),
        scratch_shapes=[pltpu.VMEM((rows, cols), x.dtype), pltpu.SemaphoreType.DMA, pltpu.SemaphoreType.DMA],
        compiler_params=pltpu.CompilerParams(collective_id=1, has_side_effects=True),
        name='swap_rows',
    )(x)


def ring_step(i):
    return 1 + 2 * i - 3 * (i // 2)


def block_kernel(scale2, q_ref, kt_ref, v_ref, x_ref, st_ref, s_ref, g_ref, wo_hbm, wg_hbm, wu_hbm, wd_hbm, y_ref, qb, kb, vb, so, ob, wo, part, jb, acc_s, m_s, l_s,
                 h_ref, send, recv, res, back, wg, wu, wd, w_sem, hop, s_ss, s_rs, r_ss, r_rs,
                 wo_sem, q_ss, k_ss, v_ss, o_ss, q_rs, kx_rs, vx_rs, o_rs, k_rs, v_rs, kp_rs, vp_rs, kd_ss, vd_ss, kf_ss, vf_ss, kp_ss, vp_ss, j_ss, j_rs):
    cp, c = lax.axis_index('cp'), lax.axis_index('tp')
    x, y, z = cp % 4, (cp // 4) % 4, cp // 16
    g = z * 4 + y
    seg = kt_ref.shape[-1]
    half = seg // 2
    heads = qb.shape[0]
    me = cp * 2 + c

    def dev(xx, yy, zz, t):
        return (0, (zz % 4) * 16 + (yy % 4) * 4 + xx % 4, t)

    barrier = pltpu.get_barrier_semaphore()
    for d in STEPS:
        for t in range(2):
            pl.semaphore_signal(barrier, inc=1, device_id=dev(x + d, y, z, t), device_id_type=MESH)
        pl.semaphore_signal(barrier, inc=1, device_id=dev(x, y + d, z, c), device_id_type=MESH)
        pl.semaphore_signal(barrier, inc=1, device_id=dev(x, y, z + d, c), device_id_type=MESH)
    pl.semaphore_signal(barrier, inc=1, device_id=dev(x, y, z, 1 - c), device_id_type=MESH)
    wo_loads = [pltpu.make_async_copy(wo_hbm.at[:, hh], wo.at[hh], wo_sem.at[hh]) for hh in range(heads)]
    for copy in wo_loads:
        copy.start()
    loads = [pltpu.make_async_copy(a, b, w_sem.at[i]) for i, (a, b) in enumerate(((wg_hbm, wg), (wu_hbm, wu), (wd_hbm, wd)))]
    for copy in loads:
        copy.start()
    pl.semaphore_wait(barrier, 13)
    for d in STEPS:
        pl.semaphore_signal(hop.at[0], inc=1, device_id=dev(x, y + d, z, c), device_id_type=MESH)

    def move(src, dst, ssem, rsem, xx, t, start):
        here = (xx == x) & (t == c)
        far = pltpu.make_async_remote_copy(src_ref=src, dst_ref=dst, send_sem=ssem, recv_sem=rsem, device_id=dev(xx, y, z, t), device_id_type=MESH)

        @pl.when(jnp.logical_not(here))
        def _():
            if start:
                far.start()
            else:
                far.wait_send()

        if start:
            @pl.when(here)
            def _():
                pltpu.make_async_copy(src, dst, rsem).start()

    def exchange(start):
        for j in range(2):
            for t in range(2):
                i = j * 2 + t
                move(kt_ref.at[j, t], kb.at[t, g, x], k_ss.at[i], kx_rs, 2 * c + j, t, start)
                move(v_ref.at[j, t], vb.at[t, g, x], v_ss.at[i], vx_rs, 2 * c + j, t, start)
        for hh in range(heads):
            for j in range(2):
                for t in range(2):
                    i = j * 2 + t
                    move(q_ref.at[:, pl.ds((i * heads + hh) * 128, 128)], qb.at[hh, x], q_ss.at[hh, i], q_rs.at[hh], 2 * c + j, t, start)

    def arrived(ref, sem):
        pltpu.make_async_copy(ref, ref, sem).wait()

    def push(buf, gg, yy, zz, t, ssem, rsem):
        pltpu.make_async_remote_copy(src_ref=buf.at[c, gg], dst_ref=buf.at[c, gg], send_sem=ssem, recv_sem=rsem.at[gg], device_id=dev(x, yy, zz, t), device_id_type=MESH).start()

    def to_partner(gg):
        push(kb, gg, y, z, 1 - c, kp_ss, kp_rs)
        push(vb, gg, y, z, 1 - c, vp_ss, vp_rs)

    def group(dy, dz):
        return ((z + 4 - dz) % 4) * 4 + (y + 4 - dy) % 4

    def pass_direct(i):
        d = ring_step(i)
        gy, gz = group(d, 0), group(0, d)
        for gg in (gy, gz):
            arrived(kb.at[c, gg], k_rs.at[gg])
            arrived(vb.at[c, gg], v_rs.at[gg])
        for e in STEPS:
            push(kb, gy, y, z + e, c, kf_ss, k_rs)
            push(vb, gz, y + e, z, c, vf_ss, v_rs)
        to_partner(gy)
        to_partner(gz)

    exchange(True)
    arrived(kb.at[c, g], kx_rs)
    arrived(vb.at[c, g], vx_rs)
    for d in STEPS:
        push(kb, g, y + d, z, c, kd_ss, k_rs)
        push(vb, g, y + d, z, c, vd_ss, v_rs)
        push(kb, g, y, z + d, c, kd_ss, k_rs)
        push(vb, g, y, z + d, c, vd_ss, v_rs)
        if d == 1:
            to_partner(g)

    rows = 2 * seg

    def q_unit(qs, hh, xp):
        parts = [qb[hh, xx, pl.ds(pl.multiple_of(qs * seg, seg), seg), :] for xx in (2 * xp, 2 * xp + 1)]
        return jnp.concatenate(parts, axis=0)

    def tiles(todo):
        def score(item):
            ggs, qs, h, masked, first, hh, xp = item
            kt = jnp.concatenate([kb[h, gg, i] for gg in ggs for i in range(4)], axis=1)
            return jnp.dot(q_unit(qs, hh, xp), kt, preferred_element_type=jnp.float32)

        s_next = score(todo[0])
        for n, (ggs, qs, h, masked, first, hh, xp) in enumerate(todo):
            s = s_next
            keys = s.shape[1]
            if n + 1 < len(todo):
                s_next = score(todo[n + 1])
            if masked:
                col = lax.broadcasted_iota(jnp.int32, (rows, keys), 1)
                row = lax.broadcasted_iota(jnp.int32, (rows, keys), 0) + xp * rows
                ck, cq = col // seg, row // seg
                before = (ck < cq) if h == 0 else (ck > cq)
                s = jnp.where(before | ((ck == cq) & (col % seg <= row % seg)), s, NEG)
            at = pl.ds(xp * rows, rows)
            m_new = jnp.broadcast_to(jnp.max(s, axis=1, keepdims=True) * scale2, (rows, 128))
            if not first:
                m_prev = m_s[qs, hh, at]
                m_new = jnp.maximum(m_prev, m_new)
                alpha = jnp.exp2(m_prev - m_new)
            m_s[qs, hh, at] = m_new
            ps = [jnp.exp2(s[:, i * 128:(i + 1) * 128] * scale2 - m_new) for i in range(keys // 128)]
            lp = ps[0]
            for v in ps[1:]:
                lp = lp + v
            p = jnp.concatenate([v.astype(jnp.bfloat16) for v in ps], axis=1)
            val = jnp.concatenate([vb[h, gg].reshape(4 * seg, 128) for gg in ggs], axis=0)
            pv = jnp.dot(p, val, preferred_element_type=jnp.float32)
            if first:
                l_s[qs, hh, at] = lp
                acc_s[qs, hh, at] = pv
            else:
                l_s[qs, hh, at] = l_s[qs, hh, at] * alpha + lp
                acc_s[qs, hh, at] = acc_s[qs, hh, at] * alpha + pv

    def ready(gg):
        arrived(kb.at[1 - c, gg], kp_rs.at[gg])
        arrived(vb.at[1 - c, gg], vp_rs.at[gg])

    def later(ggs, hh):
        todo = []
        for n in range(0, len(ggs), 2):
            pair = ggs[n:n + 2]
            todo += [(pair, 1, 0, False, False, hh, xp) for xp in range(2)]
            for gg in pair:
                h = (gg > g).astype(jnp.int32)
                todo += [([gg], h, h, False, False, hh, xp) for xp in range(2)]
        return todo

    def corner(i):
        return group(ring_step(i // 3), ring_step(i % 3))

    def pass_corner(i):
        gg = corner(i)
        arrived(kb.at[c, gg], k_rs.at[gg])
        arrived(vb.at[c, gg], v_rs.at[gg])
        to_partner(gg)

    pass_direct(0)
    pl.semaphore_wait(hop.at[0], 3)
    for d in STEPS:
        pl.semaphore_signal(hop.at[1], inc=1, device_id=dev(x, y, z + d, c), device_id_type=MESH)
    ready(g)
    near = [group(1, 0), group(0, 1), group(3, 0), group(0, 3)]

    def first_phase(hh, _):
        arrived(qb.at[hh], q_rs.at[hh])
        tiles([([g], qs, hf, masked, first, hh, xp) for qs, hf, masked, first in ((1, 0, False, True), (0, 0, True, True), (1, 1, True, False)) for xp in range(2)])

        @pl.when(hh == 0)
        def _():
            pass_direct(1)
            for gg in near:
                ready(gg)

        @pl.when(hh == 1)
        def _():
            pass_direct(2)

        tiles(later(near, hh))
        return 0

    lax.fori_loop(0, heads, first_phase, 0)

    pass_corner(0)
    pass_corner(1)

    def second_phase(i, _):
        first_c = corner(jnp.maximum(2 * i - 2, 0))
        second_c = corner(jnp.maximum(2 * i - 1, 0))
        pair = [jnp.where(i == 0, group(2, 0), first_c), jnp.where(i == 0, group(0, 2), second_c)]
        for gg in pair:
            ready(gg)
        tiles([u for hh in range(heads // 2) for u in later(pair, hh)])
        pass_corner(2 * i + 2)
        pass_corner(2 * i + 3)
        tiles([u for hh in range(heads // 2, heads) for u in later(pair, hh)])
        return 0

    lax.fori_loop(0, 3, second_phase, 0)

    pass_corner(8)
    last = [corner(i) for i in range(4, 9)]
    for gg in last:
        ready(gg)

    def o_move(hh, start):
        for i in range(4):
            move(so.at[hh, i], ob.at[hh, (x % 2) * 2 + c], o_ss.at[hh, i], o_rs.at[hh], i, x // 2, start)

    def third_phase(hh, _):
        tiles(later(last, hh))
        for qs in range(2):
            for xp in range(2):
                at = pl.ds(xp * rows, rows)
                out = (acc_s[qs, hh, at] / jnp.sum(l_s[qs, hh, at], axis=1, keepdims=True)).astype(so.dtype)
                for n in range(2):
                    so[hh, 2 * xp + n, qs * seg:(qs + 1) * seg, :] = out[n * seg:(n + 1) * seg]
        o_move(hh, True)
        return 0

    lax.fori_loop(0, heads, third_phase, 0)

    n_blk = 4
    wide = part.shape[3] // n_blk

    def cols(b):
        return pl.ds(b * wide, wide)

    def joined(b):
        return pltpu.make_async_remote_copy(src_ref=part.at[:, 1 - c, :, cols(b)], dst_ref=jb.at[:, :, cols(b)], send_sem=j_ss.at[b], recv_sem=j_rs.at[b], device_id=dev(x, y, z, 1 - c), device_id_type=MESH)

    for hh in range(heads):
        wo_loads[hh].wait()
        arrived(ob.at[hh], o_rs.at[hh])
        o_rows = jnp.concatenate([ob[hh, i] for i in range(4)], axis=1)
        for b in range(n_blk):
            term = jnp.dot(o_rows, wo[hh, :, :, b * wide:(b + 1) * wide].reshape(4 * 128, wide), preferred_element_type=jnp.float32)
            at = slice(b * wide, (b + 1) * wide)
            term = term.reshape(2, 2, half, wide)
            part[:, :, :, at] = term if hh == 0 else part[:, :, :, at] + term
            if hh == heads - 1:
                joined(b).start()
    for b in range(n_blk):
        joined(b).wait()
        at = slice(b * wide, (b + 1) * wide)
        for n in range(2):
            own_rows = slice(n * half, (n + 1) * half)
            h_ref[own_rows, at] = (x_ref[own_rows, at].astype(jnp.float32) + (part[n, c, :, at] + jb[n, :, at])).astype(h_ref.dtype)

    n_dev, cap, width = send.shape
    n_grp = s_rs.shape[0]
    per = n_dev // n_grp
    rows = per * cap
    for copy in loads:
        copy.wait()

    def pack(lo):
        at = lax.broadcasted_iota(jnp.int32, (seg, st_ref.shape[1]), 0) + lo * seg
        pick = (at == st_ref[0:1, :]) | (at == st_ref[1:2, :])
        out = jnp.dot(pick.astype(jnp.bfloat16), h_ref[...], preferred_element_type=jnp.float32)
        send[pl.ds(lo * (seg // cap), seg // cap)] = out.astype(jnp.bfloat16).reshape(seg // cap, cap, width)

    for lo in range(n_dev * cap // seg):
        pack(lo)

    pl.semaphore_wait(hop.at[1], 3)

    def peer(k, sign):
        j = (k * 91) % n_dev
        xx = (x + sign * ((j // 2) % 4)) % 4
        yy = (y + sign * ((j // 8) % 4)) % 4
        zz = (z + sign * (j // 32)) % 4
        return zz * 16 + yy * 4 + xx, (c + j) % 2

    def give(k, _):
        pc, t = peer(k, 1)
        pltpu.make_async_remote_copy(src_ref=send.at[pc * 2 + t], dst_ref=recv.at[k], send_sem=s_ss, recv_sem=s_rs.at[k // per], device_id=(0, pc, t), device_id_type=MESH).start()
        return 0

    own = pltpu.make_async_copy(send.at[me], recv.at[0], s_rs.at[0])
    own.start()
    lax.fori_loop(1, n_dev, give, 0)

    def answer(k, _):
        pc, t = peer(k, 3)
        pltpu.make_async_remote_copy(src_ref=res.at[k], dst_ref=back.at[me], send_sem=r_ss, recv_sem=r_rs, device_id=(0, pc, t), device_id_type=MESH).start()
        return 0

    def group(i, _):
        part = recv.at[pl.ds(i * per, per)]
        pltpu.make_async_copy(part, part, s_rs.at[i]).wait()
        rows_in = part[...].reshape(rows, width)
        gate = jnp.dot(rows_in, wg[...], preferred_element_type=jnp.float32)
        up = jnp.dot(rows_in, wu[...], preferred_element_type=jnp.float32)
        act = (jax.nn.silu(gate) * up).astype(jnp.bfloat16)
        out = jnp.dot(act, wd[...], preferred_element_type=jnp.float32)
        res[pl.ds(i * per, per)] = out.astype(jnp.bfloat16).reshape(per, cap, width)
        lax.fori_loop(jnp.maximum(i * per, 1), (i + 1) * per, answer, 0)
        return 0

    lax.fori_loop(0, n_grp, group, 0)
    own_back = pltpu.make_async_copy(res.at[0], back.at[me], r_rs)
    own_back.start()
    pltpu.make_async_copy(back, back, r_rs).wait()
    all_back = back[...].reshape(n_dev * cap, width)
    at = lax.broadcasted_iota(jnp.int32, (s_ref.shape[0], n_dev * cap), 1)
    total = h_ref[...].astype(jnp.float32)
    moe = None
    for j in range(2):
        pick = (at == s_ref[:, j:j + 1]).astype(jnp.bfloat16)
        term = g_ref[:, j:j + 1] * jnp.dot(pick, all_back, preferred_element_type=jnp.float32)
        moe = term if moe is None else moe + term
    y_ref[...] = (total + moe).astype(y_ref.dtype)
    most = send.at[pl.ds(1, n_dev - 1)]
    pltpu.make_async_copy(most, most, s_ss).wait()
    pltpu.make_async_copy(most, most, r_ss).wait()
    exchange(False)
    for hh in range(heads):
        o_move(hh, False)
    arrived(kb.at[0, pl.ds(0, 6)], kd_ss)
    arrived(vb.at[0, pl.ds(0, 6)], vd_ss)
    arrived(kb.at[0, pl.ds(0, 9)], kf_ss)
    arrived(vb.at[0, pl.ds(0, 9)], vf_ss)
    arrived(kb.at[0], kp_ss)
    arrived(vb.at[0], vp_ss)


def block(q, kt, val, x_blk, slot_ids, gates, w_o, w_gate, w_up, w_down, cap):
    rows, cols = q.shape
    seg = kt.shape[-1]
    heads = cols // 512
    tok_dev, d_model = x_blk.shape
    ff = w_gate.shape[1]
    n_dev = 4 * tok_dev // cap
    n_grp = 8
    dma = pltpu.SemaphoreType.DMA
    bf, f32 = jnp.bfloat16, jnp.float32
    vm = pl.BlockSpec(memory_space=pltpu.VMEM)
    hbm = pl.BlockSpec(memory_space=pltpu.HBM)
    buf = pltpu.VMEM((n_dev, cap, d_model), bf)
    return pl.pallas_call(
        functools.partial(block_kernel, (128 ** -0.5) * math.log2(math.e)),
        out_shape=jax.ShapeDtypeStruct(x_blk.shape, bf),
        in_specs=[vm] * 7 + [hbm] * 4,
        out_specs=vm,
        scratch_shapes=[
            pltpu.VMEM((heads, 4, rows, 128), bf),
            pltpu.VMEM((2, 16, 4, seg, 128), bf),
            pltpu.VMEM((2, 16, 4, seg, 128), bf),
            pltpu.VMEM((heads, 4, rows, 128), bf),
            pltpu.VMEM((heads, 4, rows, 128), bf),
            pltpu.VMEM((heads, 4, 128, d_model), bf),
            pltpu.VMEM((2, 2, tok_dev // 2, d_model), f32),
            pltpu.VMEM((2, tok_dev // 2, d_model), f32),
            pltpu.VMEM((2, heads, 4 * seg, 128), f32),
            pltpu.VMEM((2, heads, 4 * seg, 128), f32),
            pltpu.VMEM((2, heads, 4 * seg, 128), f32),
            pltpu.VMEM(x_blk.shape, bf),
            buf, buf, buf, buf,
            pltpu.VMEM((d_model, ff), bf), pltpu.VMEM((d_model, ff), bf), pltpu.VMEM((ff, d_model), bf),
            dma((3,)), pltpu.SemaphoreType.REGULAR((2,)), dma, dma((n_grp,)), dma, dma,
            dma((heads,)), dma((heads, 4)), dma((4,)), dma((4,)), dma((heads, 4)),
            dma((heads,)), dma, dma, dma((heads,)),
            dma((16,)), dma((16,)), dma((16,)), dma((16,)),
            dma, dma, dma, dma, dma, dma, dma((4,)), dma((4,)),
        ],
        compiler_params=pltpu.CompilerParams(collective_id=3, has_side_effects=True, vmem_limit_bytes=60 * 1024 * 1024),
        name='ring_block',
    )(q, kt, val, x_blk, slot_ids.T, slot_ids, gates, w_o.reshape(4, heads, 128, d_model), w_gate, w_up, w_down)


def solution(mesh):
    cp_size = mesh.shape['cp']
    tp_size = mesh.shape['tp']
    num_devs = cp_size * tp_size
    row_spec = P(('data', 'cp', 'tp'), None)
    head_spec = P(None, 'tp', None)
    wo_spec = P('tp', None, None)
    expert_spec = P(('cp', 'tp'), None, None)

    def device_fn(x_blk, w_q, w_k, w_v, w_o, idx_blk, gate_blk, w_gate, w_up, w_down):
        tok_dev, d_model = x_blk.shape
        exp_local = w_gate.shape[0]
        num_exp = exp_local * num_devs
        capacity = 4 * tok_dev // num_exp

        x_rows = swap_rows(x_blk)
        x_seg = x_rows.reshape(2, tok_dev, d_model)
        key_t = jnp.einsum('mnc,hsm->nhcs', w_k, x_seg, preferred_element_type=jnp.float32).astype(jnp.bfloat16)
        val = jnp.einsum('hsm,mnc->nhsc', x_seg, w_v, preferred_element_type=jnp.float32).astype(jnp.bfloat16)
        queries = jnp.dot(x_rows, w_q.reshape(d_model, -1), preferred_element_type=jnp.float32).astype(jnp.bfloat16)
        flat_ids = idx_blk.reshape(-1)
        onehot = (flat_ids[:, None] == jnp.arange(num_exp)[None, :]).astype(jnp.int32)
        slot_pos = jnp.sum(jnp.cumsum(onehot, axis=0) * onehot, axis=1) - 1
        slot_ids = (flat_ids * capacity + slot_pos).reshape(tok_dev, 2)
        return block(queries, key_t, val, x_blk, slot_ids, gate_blk, w_o, w_gate[0], w_up[0], w_down[0], capacity)

    return jax.shard_map(device_fn, mesh=mesh, in_specs=(row_spec, head_spec, head_spec, head_spec, wo_spec, row_spec, row_spec, expert_spec, expert_spec, expert_spec), out_specs=row_spec, check_vma=False)
```

time: 178 us -> 172 us (0.966)
  local copies, waits for them, and re-layouts: 6.77 us -> 4.09 us
    unnamed x12 -> x16, local copies, waits for them, and re-layouts: 4.72 us -> 2.76 us
    pallas_call x2 -> x1, Pallas kernels: 153 us -> 153 us  [block(): pl.pallas_call(functools.partial(block_kernel, 128 ** (-0.5) * math.log2(...]
where the time goes in v4:
time: 172 us
  Pallas kernels  158 us (92%)
  matrix products  9.45 us (5%)
  local copies, waits for them, and re-layouts  4.09 us (2%)
    pallas_call x1, Pallas kernels, block(): pl.pallas_call(functools.partial(block_kernel, 128 ** (-0.5) * math.log2(...  153 us
    dot_general x1, matrix products, device_fn(): jnp.dot(x_rows, w_q.reshape(d_model, -1), preferred_element_type=jnp.floa...  7.18 us
    pallas_call x1, Pallas kernels, swap_rows(): pl.pallas_call(swap_kernel, out_shape=jax.ShapeDtypeStruct((2 * rows, col...  5.11 us

profile of v4, /device:TPU:1, one launch (start us, length us, event | category | flops | bytes accessed | tf_op | source)
XLA Modules:
  0.0 172.1 jit_solution(12765940728884809027)
XLA Ops:
  0.0 0.0 copy-start
  0.0 5.1 %swap_rows.1 = bf16[256,2048]{1,0:T(8,128)(2,1)} custom-call(bf16[128,2048]{1,0:T(8,128)(2,1)} %x_ref.3), custom_call_target="tpu_custom_call" | custom-call | tf_op jit(solution)/shard_map/swap_rows/pallas_call | solution.py:38
  5.1 0.0 copy-start.1
  5.1 0.0 copy-start.5
  5.1 0.0 copy-start.3
  5.2 0.0 copy-start.4
  5.2 7.2 %fusion.3.q_ref = bf16[256,2048]{1,0:T(8,128)(2,1)} fusion(bf16[256,2048]{1,0:T(8,128)(2,1)} %swap_rows.1, bf16[256,8,16,128]{3,2,1,0:T(8,128)(2,1)} %bitcast.45), kind=kOutput, calls=%fused_computation.3 | convolution fusion | flops 2148007936 | bytes 10485760 | tf_op jit(solution)/shard_map/dot_general | solution.py:449
  12.4 0.0 copy-done
  12.4 0.0 copy-done.1
  12.4 1.2 fusion.6.kt_ref
  13.5 0.0 copy-done.5
  13.5 1.1 fusion.7.v_ref
  14.6 0.0 copy-done.3
  14.6 0.1 copy.39
  14.8 0.1 copy.35
  14.9 0.1 eq.29
  15.0 0.1 copy.37
  15.1 0.2 fusion.10
  15.4 0.1 eq.25
  15.6 0.2 fusion.11
  15.8 0.1 sub.7
  15.9 0.0 copy-start.2
  15.9 0.7 copy.40.st_ref
  16.6 0.0 copy-done.4
  16.6 0.7 copy.41.g_ref
  17.3 0.0 copy-done.2
  17.3 152.9 %ring_block.1 = bf16[128,2048]{1,0:T(8,128)(2,1)} custom-call(bf16[256,2048]{1,0:T(8,128)(2,1)} %fusion.3.q_ref, bf16[2,2,128,128]{3,2,1,0:T(8,128)(2,1)} %fusion.6.kt_ref, bf16[2,2,128,128]{3,2,1,0:T(8,128)(2,1)} %fusion.7.v_ref, bf16[128,2048]{1,0:T(8,128)(2,1)} %x_ref.3, s32[2,128]{1,0:T(2,128)} %copy.40.st_ref, s32[128,2]{1,0:T(8,128)} %copy-done.2, ...), custom_call_target="tpu_custom_call" | custom-call | tf_op jit(solution)/shard_map/ring_block/pallas_call | solution.py:399
  170.2 1.9 %copy.62 = bf16[128,2048]{1,0:T(8,128)(2,1)} copy(bf16[128,2048]{1,0:T(8,128)(2,1)} %ring_block.1) | data formatting | bytes 1048576
  (9 shorter events, 0.1 us)
Async XLA Ops:
  0.0 12.4 %copy-start = (bf16[2048,2,128]{2,1,0:T(2,128)(2,1)S(1)}, bf16[2048,2,128]{2,1,0:T(2,128)(2,1)}, u32[]{:S(2)}) copy-start(bf16[2048,2,128]{2,1,0:T(2,128)(2,1)} %param.12) | copy-start | bytes 3145732
  5.1 7.2 %copy-start.1 = (bf16[256,2048]{1,0:T(8,128)(2,1)S(1)}, bf16[256,2048]{1,0:T(8,128)(2,1)}, u32[]{:S(2)}) copy-start(bf16[256,2048]{1,0:T(8,128)(2,1)} %swap_rows.1) | copy-start | bytes 3145732
  5.1 8.4 %copy-start.5 = (bf16[2048,2,128]{2,1,0:T(2,128)(2,1)S(1)}, bf16[2048,2,128]{2,1,0:T(2,128)(2,1)}, u32[]{:S(2)}) copy-start(bf16[2048,2,128]{2,1,0:T(2,128)(2,1)} %param.13) | copy-start | bytes 3145732
  5.1 9.5 %copy-start.3 = (s32[128,2]{0,1:T(2,128)S(1)}, s32[128,2]{0,1:T(2,128)}, u32[]{:S(2)}) copy-start(s32[128,2]{0,1:T(2,128)} %param.15) | copy-start | bytes 3076
  5.2 11.5 %copy-start.4 = (f32[128,2]{0,1:T(2,128)S(1)}, f32[128,2]{0,1:T(2,128)}, u32[]{:S(2)}) copy-start(f32[128,2]{0,1:T(2,128)} %param.16) | copy-start | bytes 3076
  15.9 1.4 copy-start.2

commit v5 on v4

--- a/solution.py
+++ b/solution.py
@@ -213,7 +213,6 @@
         arrived(vb.at[c, gg], v_rs.at[gg])
         to_partner(gg)
 
-    pass_direct(0)
     pl.semaphore_wait(hop.at[0], 3)
     for d in STEPS:
         pl.semaphore_signal(hop.at[1], inc=1, device_id=dev(x, y, z + d, c), device_id_type=MESH)
@@ -226,6 +225,7 @@
 
         @pl.when(hh == 0)
         def _():
+            pass_direct(0)
             pass_direct(1)
             for gg in near:
                 ready(gg)
@@ -422,7 +422,7 @@
             dma((16,)), dma((16,)), dma((16,)), dma((16,)),
             dma, dma, dma, dma, dma, dma, dma((4,)), dma((4,)),
         ],
-        compiler_params=pltpu.CompilerParams(collective_id=3, has_side_effects=True, vmem_limit_bytes=60 * 1024 * 1024),
+        compiler_params=pltpu.CompilerParams(collective_id=3, has_side_effects=True, vmem_limit_bytes=52 * 1024 * 1024),
         name='ring_block',
     )(q, kt, val, x_blk, slot_ids.T, slot_ids, gates, w_o.reshape(4, heads, 128, d_model), w_gate, w_up, w_down)
 

time: 172 us -> 166 us (0.965)
  Pallas kernels: 158 us -> 155 us
  local copies, waits for them, and re-layouts: 4.09 us -> 1.79 us
    pallas_call x1, Pallas kernels: 153 us -> 150 us  [block(): pl.pallas_call(functools.partial(block_kernel, 128 ** (-0.5) * math.log2(...]
where the time goes in v5:
time: 166 us
  Pallas kernels  155 us (93%)
  matrix products  8.21 us (5%)
  local copies, waits for them, and re-layouts  1.79 us (1%)
    pallas_call x1, Pallas kernels, block(): pl.pallas_call(functools.partial(block_kernel, 128 ** (-0.5) * math.log2(...  150 us
    dot_general x1, matrix products, device_fn(): jnp.dot(x_rows, w_q.reshape(d_model, -1), preferred_element_type=jnp.floa...  7.24 us
    pallas_call x1, Pallas kernels, swap_rows(): pl.pallas_call(swap_kernel, out_shape=jax.ShapeDtypeStruct((2 * rows, col...  5.07 us

profile of v5, /device:TPU:1, one launch (start us, length us, event | category | flops | bytes accessed | tf_op | source)
XLA Modules:
  0.0 166.0 jit_solution(18405164970004704130)
XLA Ops:
  0.0 0.0 copy-start
  0.0 5.1 %swap_rows.1 = bf16[256,2048]{1,0:T(8,128)(2,1)} custom-call(bf16[128,2048]{1,0:T(8,128)(2,1)} %x_ref.3), custom_call_target="tpu_custom_call" | custom-call | tf_op jit(solution)/shard_map/swap_rows/pallas_call | solution.py:38
  5.1 0.0 copy-start.2
  5.1 0.0 copy-start.5
  5.1 0.0 copy-start.3
  5.1 0.0 copy-start.4
  5.1 0.0 copy-start.1
  5.1 7.2 %fusion.3.q_ref = bf16[256,2048]{1,0:T(8,128)(2,1)} fusion(bf16[256,2048]{1,0:T(8,128)(2,1)} %swap_rows.1, bf16[256,8,16,128]{3,2,1,0:T(8,128)(2,1)} %bitcast.45), kind=kOutput, calls=%fused_computation.3 | convolution fusion | flops 2148007936 | bytes 10485760 | tf_op jit(solution)/shard_map/dot_general | solution.py:449
  12.4 0.0 copy-done
  12.4 0.0 copy-done.2
  12.4 0.5 fusion.6.kt_ref
  12.9 0.0 copy-done.5
  12.9 0.4 fusion.7.v_ref
  13.4 0.0 copy-done.3
  13.4 0.1 copy.39
  13.5 0.1 copy.35
  13.6 0.1 eq.29
  13.8 0.1 copy.37
  13.9 0.2 fusion.10
  14.2 0.1 eq.25
  14.3 0.2 fusion.11
  14.5 0.1 sub.7
  14.7 0.1 copy.40.st_ref
  14.8 0.0 copy-done.4
  14.8 0.1 copy.41.g_ref
  14.9 0.0 copy-done.1
  14.9 150.3 %ring_block.1 = bf16[128,2048]{1,0:T(8,128)(2,1)S(1)} custom-call(bf16[256,2048]{1,0:T(8,128)(2,1)} %fusion.3.q_ref, bf16[2,2,128,128]{3,2,1,0:T(8,128)(2,1)S(1)} %fusion.6.kt_ref, bf16[2,2,128,128]{3,2,1,0:T(8,128)(2,1)S(1)} %fusion.7.v_ref, bf16[128,2048]{1,0:T(8,128)(2,1)S(1)} %copy-done.1, s32[2,128]{1,0:T(2,128)S(1)} %copy.40.st_ref, ...), custom_call_target="tpu_custom_call" | custom-call | tf_op jit(solution)/shard_map/ring_block/pallas_call | solution.py:399
  165.2 0.8 copy.62
  (9 shorter events, 0.1 us)
Async XLA Ops:
  0.0 12.4 %copy-start = (bf16[2048,2,128]{2,1,0:T(2,128)(2,1)S(1)}, bf16[2048,2,128]{2,1,0:T(2,128)(2,1)}, u32[]{:S(2)}) copy-start(bf16[2048,2,128]{2,1,0:T(2,128)(2,1)} %param.12) | copy-start | bytes 3145732
  5.1 7.3 %copy-start.2 = (bf16[256,2048]{1,0:T(8,128)(2,1)S(1)}, bf16[256,2048]{1,0:T(8,128)(2,1)}, u32[]{:S(2)}) copy-start(bf16[256,2048]{1,0:T(8,128)(2,1)} %swap_rows.1) | copy-start | bytes 3145732
  5.1 7.8 %copy-start.5 = (bf16[2048,2,128]{2,1,0:T(2,128)(2,1)S(1)}, bf16[2048,2,128]{2,1,0:T(2,128)(2,1)}, u32[]{:S(2)}) copy-start(bf16[2048,2,128]{2,1,0:T(2,128)(2,1)} %param.13) | copy-start | bytes 3145732
  5.1 8.3 %copy-start.3 = (s32[128,2]{0,1:T(2,128)S(1)}, s32[128,2]{0,1:T(2,128)}, u32[]{:S(2)}) copy-start(s32[128,2]{0,1:T(2,128)} %param.15) | copy-start | bytes 3076
  5.1 9.6 %copy-start.4 = (f32[128,2]{0,1:T(2,128)S(1)}, f32[128,2]{0,1:T(2,128)}, u32[]{:S(2)}) copy-start(f32[128,2]{0,1:T(2,128)} %param.16) | copy-start | bytes 3076
  5.1 9.8 %copy-start.1 = (bf16[128,2048]{1,0:T(8,128)(2,1)S(1)}, bf16[128,2048]{1,0:T(8,128)(2,1)}, u32[]{:S(2)}) copy-start(bf16[128,2048]{1,0:T(8,128)(2,1)} %x_ref.3) | copy-start | bytes 1572868
